TPU v7x, 512 devices: a whole 4x8x8 slice. The times are simulated.
512 devices in a mesh: seq: 32 (over x, y), batch: 16 (over z, core).
Axes of the slice: x: 4, y: 8, z: 8, core: 2. Of those that a mesh axis runs over, the one named last changes fastest.
Arguments:
- queries: bfloat16 [64, 4096], P('batch', 'seq'), may hold values from -210 to 210
- key_cache: bfloat16 [64, 4096, 2048], P('batch', 'seq'), may hold values from -6 to 6
- value_cache: bfloat16 [64, 4096, 2048], P('batch', 'seq'), may hold values from -12 to 12
- new_key: bfloat16 [64, 2048], P('batch'), may hold values from -6 to 6
- new_value: bfloat16 [64, 2048], P('batch'), may hold values from -12 to 12
- page_table: int32 [64, 32], P('batch', 'seq'), may hold values from 0 to 3, as said below
- counts: int32 [64, 32], P('batch', 'seq'), may hold values from 1 to 128
- offsets: int32 [64], P('batch'), may hold values from 0 to 3968
- w_out: bfloat16 [4096, 4608], P('seq', 'batch'), may hold values from -0.09375 to 0.09375
Outputs:
- projected: bfloat16 [64, 4608], P('seq', 'batch')
Inputs may be any that keep to these rules, and one draw needn't show every extreme that they name: `page_table`: for each group of 4 requests and each index along seq, the slots of that index's 1 pages of the group's requests are all different.
All inputs are finite; a program needn't handle non-finite values.
Results may differ from a plain program's by a relative error of at most 0.005.
Values may be sent and summed in bfloat16 or wider, within the bound.
No kernel may reach another device: no remote copies, remote signals or barrier semaphores. Data moves between devices by JAX's collectives and lax.ppermute only.
A program may use at most 64 MiB of HBM per device.

v0:
```python
import jax
import jax.numpy as jnp
from jax import lax
from jax.sharding import Mesh
from jax.sharding import PartitionSpec as P

HEADS = 32
KVH = 16
HD = 128
QSCALAR = 144
SEQ = ("seq_0", "seq_1")


floor_score = -1e30


def from_everyone(x, axis):
    peers = lax.axis_size(axis)
    return lax.all_to_all(jnp.broadcast_to(x[None], (peers, *x.shape)), axis, 0, 0, tiled=True)


def laid_out(blocks, dim):
    blocks = jnp.moveaxis(blocks, 0, dim)
    dims = blocks.shape
    return blocks.reshape(*dims[:dim], dims[dim] * dims[dim + 1], *dims[dim + 2 :])


def collect(x, axis, dim):
    blocks = from_everyone(x, axis)
    return laid_out(blocks, dim)


def all_in_one(x, axis):
    leaves = jax.tree.leaves(x)
    order = sorted(range(len(leaves)), key=lambda k: -leaves[k].size)
    width = (1, *leaves[order[0]].shape)[-1]
    lines = [
        jnp.pad(leaves[k].reshape(-1), (0, -leaves[k].size % width)).reshape(-1, width)
        for k in order
    ]
    both, at, found = (lax.all_gather(jnp.concatenate(lines), axis), 0, {})
    for k, line in zip(order, lines):
        slab = both[:, at : at + len(line)].reshape(len(both), -1)
        found[k] = slab[:, : leaves[k].size].reshape(-1, *leaves[k].shape)
        at += len(line)
    numbers = iter(range(len(leaves)))
    return jax.tree.map(lambda _: found[next(numbers)], x)


def merged_by_axis(x, axes, combine):
    for axis in axes:
        pieces = all_in_one(x, axis)
        x = jax.tree.map(lambda part: part[0], pieces)
        for k in range(1, lax.axis_size(axis)):
            x = combine(x, jax.tree.map(lambda part: part[k], pieces))
    return x


def cut_along(x, dim, peers):
    dims = x.shape
    blocks = x.reshape(*dims[:dim], peers, dims[dim] // peers, *dims[dim + 1 :])
    return jnp.moveaxis(blocks, dim, 0)


def sent_and_summed(x, axis, dim):
    peers = lax.axis_size(axis)
    blocks = lax.all_to_all(cut_along(x, dim, peers), axis, 0, 0, tiled=True)
    return jnp.sum(blocks, axis=0)


def on_device(
    queries, key_cache, value_cache, new_key, new_value, page_table, counts, offsets, w_out
):
    requests = queries.shape[0]
    groups = HEADS // KVH
    cycle_size = lax.axis_size(SEQ)
    cycle_place = lax.axis_index(SEQ)
    head_count = HEADS // cycle_size
    pages_here = page_table.shape[1]
    page_len = key_cache.shape[1]
    score_multiplier = QSCALAR ** (-0.5)

    def own_heads(array_in):
        return lax.dynamic_slice_in_dim(array_in, cycle_place * head_count, head_count, 1)

    all_queries = collect(queries, SEQ, 1)
    query_lattice = all_queries.reshape(requests, KVH, groups, HD)
    key_rows = jnp.take(key_cache, page_table, axis=0).reshape(
        requests, pages_here * page_len, KVH, HD
    )
    value_rows = jnp.take(value_cache, page_table, axis=0).reshape(
        requests, pages_here * page_len, KVH, HD
    )
    scores = (
        jnp.einsum("bkgd,btkd->bkgt", query_lattice, key_rows, preferred_element_type=jnp.float32)
        * score_multiplier
    )
    token_index = jnp.arange(page_len, dtype=jnp.int32)
    page_start = (cycle_place * pages_here + jnp.arange(pages_here, dtype=jnp.int32)) * page_len
    live_mask = (token_index[None, None, :] < counts[:, :, None]) & (
        page_start[None, :, None] + token_index[None, None, :] >= offsets[:, None, None]
    )
    live_mask = live_mask.reshape(requests, pages_here * page_len)[:, None, None, :]
    peak_score = jnp.max(jnp.where(live_mask, scores, floor_score), axis=-1)
    weights = jnp.where(live_mask, jnp.exp(scores - peak_score[..., None]), 0.0)
    block_total = jnp.sum(weights, axis=-1)
    block_sum = jnp.einsum(
        "bkgt,btkd->bkgd",
        weights.astype(jnp.bfloat16),
        value_rows,
        preferred_element_type=jnp.float32,
    )
    incoming_score = (
        jnp.einsum(
            "pcoz,pcz->pco",
            query_lattice,
            new_key.reshape(requests, KVH, HD),
            preferred_element_type=jnp.float32,
        )
        * score_multiplier
    )
    fresh_value = jnp.broadcast_to(
        new_value.astype(jnp.float32).reshape(requests, KVH, 1, HD), (requests, KVH, groups, HD)
    ).reshape(requests, HEADS, HD)
    flat_peak = peak_score.reshape(requests, HEADS)
    flat_total = block_total.reshape(requests, HEADS)
    flat_sum = block_sum.reshape(requests, HEADS, HD)
    flat_new = incoming_score.reshape(requests, HEADS)
    mine_new = own_heads(flat_new)
    mine_value = own_heads(fresh_value)

    def combine(earlier, later):
        top_score = jnp.maximum(earlier[0], later[0])
        left_weight = jnp.exp(earlier[0] - top_score)
        trailing_weight = jnp.exp(later[0] - top_score)
        return (
            top_score,
            earlier[1] * left_weight + later[1] * trailing_weight,
            earlier[2] * left_weight[..., None] + later[2] * trailing_weight[..., None],
        )

    merged_peak, merged_total, merged_sum = merged_by_axis(
        (flat_peak, flat_total, flat_sum), SEQ, combine
    )
    head_peak = own_heads(merged_peak)
    top_score = jnp.maximum(head_peak, mine_new)
    factor = jnp.exp(head_peak - top_score)
    own_weight = jnp.exp(mine_new - top_score)
    denominator = own_heads(merged_total) * factor + own_weight
    numerator = own_heads(merged_sum) * factor[..., None] + own_weight[..., None] * mine_value
    attention = (
        (numerator / denominator[..., None]).astype(jnp.bfloat16).reshape(requests, head_count * HD)
    )
    everyone = collect(attention, "batch", 0)
    projected = sent_and_summed(
        jnp.dot(everyone, w_out, preferred_element_type=jnp.float32), SEQ, 0
    )
    return projected.astype(jnp.bfloat16)


def solution(mesh):
    torus = Mesh(mesh.devices.reshape(4, 8, mesh.shape["batch"]), ("seq_0", "seq_1", "batch"))
    in_specs = (
        P("batch", SEQ),
        P("batch", SEQ, None),
        P("batch", SEQ, None),
        P("batch", None),
        P("batch", None),
        P("batch", SEQ),
        P("batch", SEQ),
        P("batch"),
        P(SEQ, "batch"),
    )
    out_specs = P(SEQ, "batch")
    return jax.shard_map(
        on_device, mesh=torus, in_specs=in_specs, out_specs=out_specs, check_vma=False
    )
```

profile of v0, /device:TPU:1, one launch (start us, length us, event | category | flops | bytes accessed | tf_op | source)
XLA Modules:
  0.0 110.1 jit_solution(14664414663531387777)
XLA Ops:
  0.0 1.4 %broadcast_in_dim.41 = bf16[32,4,128]{2,1,0:T(4,128)(2,1)} broadcast(bf16[4,128]{1,0:T(4,128)(2,1)} %param.11), dimensions={1,2} | broadcast | bytes 33792 | tf_op jit(solution)/shard_map/broadcast_in_dim | solution.py:19
  1.4 10.5 %all-to-all-start = ((bf16[32,4,128]{2,1,0:T(4,128)(2,1)}), bf16[32,4,128]{2,1,0:T(4,128)(2,1)S(1)}, u32[]{:S(2)}, u32[]{:S(2)}) async-start(bf16[32,4,128]{2,1,0:T(4,128)(2,1)} %broadcast_in_dim.41), calls=%async_computation | async-start | bytes 65536 | tf_op jit(solution)/shard_map/all_to_all | solution.py:19
  11.9 0.7 fusion.55
  12.6 0.7 and_bitcast_fusion
  13.3 2.0 %gather_fusion = bf16[4,128,2048]{2,1,0:T(8,128)(2,1)} fusion(bf16[4,128,2048]{2,1,0:T(8,128)(2,1)S(1)} %copy-done, s32[1024]{0:T(1024)S(1)} %pad_clamp_fusion), kind=kCustom, calls=%fused_computation.clone | custom fusion | bytes 4194320 | tf_op jit(solution)/shard_map/jit(_take)/gather | solution.py:88
  15.3 3.6 %gather_fusion.1 = bf16[4,128,2048]{2,1,0:T(8,128)(2,1)} fusion(bf16[4,128,2048]{2,1,0:T(8,128)(2,1)} %param.13, s32[1024]{0:T(1024)S(1)} %pad_clamp_fusion), kind=kCustom, calls=%fused_computation.1.clone | custom fusion | bytes 4194320 | tf_op jit(solution)/shard_map/jit(_take)/gather | solution.py:91
  18.9 2.7 %bitcast_select_fusion = (bf16[4,1,128,2048]{3,2,0,1:T(8,128)(2,1)S(1)}, bf16[4,1,128,2048]{3,2,0,1:T(8,128)(2,1)S(1)}) fusion(bf16[4,128,2048]{2,1,0:T(8,128)(2,1)} %gather_fusion.1, pred[4]{0:T(512)(128)(4,1)S(1)} %and_bitcast_fusion, bf16[4,128,2048]{2,1,0:T(8,128)(2,1)} %gather_fusion), kind=kLoop, calls=%fused_computation.2 | loop fusion | flops 2097152 | bytes 8388612 | tf_op jit(solution)/shard_map/jit(_take)/select_n | solution.py:91
  21.6 0.1 fusion.33
  21.7 2.0 %copy.46 = bf16[64,8,16,128]{3,2,1,0:T(8,128)(2,1)} copy(bf16[64,8,16,128]{3,1,2,0:T(8,128)(2,1)S(1)} %bitcast.206) | data formatting | bytes 4194304
  23.7 1.9 %copy.47 = bf16[64,8,16,128]{3,2,1,0:T(8,128)(2,1)} copy(bf16[64,8,16,128]{3,1,2,0:T(8,128)(2,1)S(1)} %bitcast.205) | data formatting | bytes 4194304
  25.7 2.9 %select_reduce_fusion = (f32[4,16,2]{2,1,0:T(8,128)S(1)}, f32[4,16,128,2]{2,3,1,0:T(2,128)S(1)}) fusion(pred[4,128]{1,0:T(4,128)(4,1)S(1)} %fusion.33, bf16[4,16,2,128]{3,2,1,0:T(2,128)(2,1)S(1)} %bitcast.222, bf16[4,128,16,128]{3,2,1,0:T(8,128)(2,1)} %bitcast.208), kind=kOutput, calls=%fused_computation.30 | convolution fusion | flops 4243328 | bytes 2196480 | tf_op jit(solution)/shard_map/bkgd,btkd->bkgt/dot_general | solution.py:95
  28.5 0.2 reshape.749
  28.7 0.3 bitcast_reduce_fusion
  29.0 2.3 %fusion = f32[4,16,2,128]{3,2,1,0:T(2,128)S(1)} fusion(bf16[4,128,16,128]{3,2,1,0:T(8,128)(2,1)} %bitcast.207, f32[4,16,128,2]{2,3,1,0:T(2,128)S(1)} %get-tuple-element.67, pred[4,128]{1,0:T(4,128)(4,1)S(1)} %fusion.33, f32[4,16,2]{2,1,0:T(8,128)S(1)} %get-tuple-element.66), kind=kOutput, calls=%fused_computation.4 | convolution fusion | flops 4243456 | bytes 2229248 | tf_op jit(solution)/shard_map/bkgt,btkd->bkgd/dot_general | solution.py:107
  31.3 0.1 reshape.750
  31.4 10.3 %all-gather.2 = f32[4,130,128]{2,1,0:T(8,128)S(1)} all-gather(f32[1,130,128]{2,1,0:T(8,128)S(1)} %maximum_bitcast_fusion), channel_id=2, replica_groups=mesh['seq_0'=4,'seq_1'=8,'batch'=16] {'seq_0'}, dimensions={0}, use_global_device_ids=true | all-gather | bytes 332800 | tf_op jit(solution)/shard_map/all_gather | solution.py:41
  41.8 0.2 fusion.10
  42.0 20.3 %all-gather.3 = f32[8,130,128]{2,1,0:T(8,128)S(1)} all-gather(f32[1,130,128]{2,1,0:T(8,128)S(1)} %maximum_bitcast_fusion.1), channel_id=3, replica_groups=mesh['seq_0'=4,'seq_1'=8,'batch'=16] {'seq_1'}, dimensions={0}, use_global_device_ids=true | all-gather | bytes 599040 | tf_op jit(solution)/shard_map/all_gather | solution.py:41
  62.4 0.1 squeeze.133
  62.5 0.1 squeeze.134
  62.5 0.1 squeeze.136
  62.6 0.1 squeeze.138
  62.7 0.1 squeeze.140
  62.8 0.1 squeeze.142
  62.9 0.1 squeeze.144
  63.0 0.1 squeeze.146
  63.0 0.1 squeeze.148
  63.1 0.1 squeeze.149
  63.2 0.1 squeeze.150
  63.3 0.1 squeeze.151
  63.4 0.1 squeeze.152
  63.5 0.1 squeeze.153
  63.5 0.1 squeeze.154
  63.6 0.1 squeeze.155
  63.7 0.2 fusion.58
  63.9 0.2 copy.43
  64.2 0.1 copy.45
  64.3 0.1 constant_dynamic-slice_fusion.4
  64.4 0.1 constant_dynamic-slice_fusion.1
  64.5 0.1 constant_dynamic-slice_fusion.7
  64.5 0.2 fusion.53
  64.8 0.2 multiply_add_fusion
  65.0 0.1 divide_convert_fusion
  65.2 27.1 %all_to_all.15 = bf16[16,4,128]{2,1,0:T(4,128)(2,1)S(1)} all-to-all(bf16[16,4,128]{2,1,0:T(4,128)(2,1)S(1)} %broadcast_in_dim.48), channel_id=1, replica_groups=mesh['seq_0'=4,'seq_1'=8,'batch'=16] {'batch'}, dimensions={0} | all-to-all | bytes 32768 | tf_op jit(solution)/shard_map/all_to_all | solution.py:19
  92.3 0.2 fusion.7
  92.4 0.1 copy.41
  92.5 17.0 %all_to_all.16 = f32[32,2,288]{2,1,0:T(2,128)S(1)} all-to-all(f32[32,2,288]{2,1,0:T(2,128)S(1)} %copy.41), channel_id=1, replica_groups=mesh['seq_0'=4,'seq_1'=8,'batch'=16] {'seq_0','seq_1'}, dimensions={0} | all-to-all | bytes 147456 | tf_op jit(solution)/shard_map/all_to_all | solution.py:67
  109.5 0.6 reduce_sum.19
  (33 shorter events, 0.3 us)
Async XLA Ops:
  0.0 13.3 %copy-start = (bf16[4,128,2048]{2,1,0:T(8,128)(2,1)S(1)}, bf16[4,128,2048]{2,1,0:T(8,128)(2,1)}, u32[]{:S(2)}) copy-start(bf16[4,128,2048]{2,1,0:T(8,128)(2,1)} %param.12) | copy-start | bytes 6291460
  1.4 24.2 %all-to-all-start = ((bf16[32,4,128]{2,1,0:T(4,128)(2,1)}), bf16[32,4,128]{2,1,0:T(4,128)(2,1)S(1)}, u32[]{:S(2)}, u32[]{:S(2)}) async-start(bf16[32,4,128]{2,1,0:T(4,128)(2,1)} %broadcast_in_dim.41), calls=%async_computation | async-start | bytes 65536 | tf_op jit(solution)/shard_map/all_to_all | solution.py:19
  15.3 3.6 %copy-start.2 = (bf16[4,2048]{1,0:T(4,128)(2,1)S(1)}, bf16[4,2048]{1,0:T(4,128)(2,1)}, u32[]{:S(2)}) copy-start(bf16[4,2048]{1,0:T(4,128)(2,1)} %param.15) | copy-start | bytes 49156
  18.9 2.7 %copy-start.4 = (s32[4,1]{0,1:T(1,128)S(1)}, s32[4,1]{0,1:T(1,128)}, u32[]{:S(2)}) copy-start(s32[4,1]{0,1:T(1,128)} %param.17) | copy-start | bytes 52
  18.9 2.7 %copy-start.5 = (s32[4]{0:T(128)S(1)}, s32[4]{0:T(128)}, u32[]{:S(2)}) copy-start(s32[4]{0:T(128)} %param.18) | copy-start | bytes 52
  23.7 1.9 %copy-start.3 = (bf16[4,2048]{1,0:T(4,128)(2,1)S(1)}, bf16[4,2048]{1,0:T(4,128)(2,1)}, u32[]{:S(2)}) copy-start(bf16[4,2048]{1,0:T(4,128)(2,1)} %param.14) | copy-start | bytes 49156
  31.3 61.0 %copy-start.1 = (bf16[128,288]{0,1:T(8,128)(2,1)S(1)}, bf16[128,288]{0,1:T(8,128)(2,1)}, u32[]{:S(2)}) copy-start(bf16[128,288]{0,1:T(8,128)(2,1)} %param.19) | copy-start | bytes 221188
where the time goes:
time: 111 us; the launch traced here: 110 us
  blocking collectives  74.7 us (67%)
  local copies, waits for them, and re-layouts  13.3 us (12%)
  starting transfers between devices  10.5 us (9%)
  other arithmetic  5.79 us (5%)
  matrix products  5.52 us (5%)
    all_gather x2, blocking collectives, all_in_one(): both, at, found = (lax.all_gather(jnp.concatenate(lines), axis), 0, {})  30.6 us
    all_to_all x1, blocking collectives, from_everyone(): lax.all_to_all(jnp.broadcast_to(x[None], (peers, *x.shape)), axis, 0, 0,...  27.1 us
    all_to_all x1, blocking collectives, sent_and_summed(): blocks = lax.all_to_all(cut_along(x, dim, peers), axis, 0, 0, tiled=True)  17 us
    all_to_all x1, starting transfers between devices, from_everyone(): lax.all_to_all(jnp.broadcast_to(x[None], (peers, *x.shape)), axis, 0, 0,...  10.5 us
    unnamed x17, local copies, waits for them, and re-layouts  4.03 us
    gather x1, local copies, waits for them, and re-layouts, on_device(): jnp.take(value_cache, page_table, axis=0)  3.63 us
    dot_general x1, matrix products, on_device(): jnp.einsum('bkgd,btkd->bkgt', query_lattice, key_rows, preferred_element_...  2.86 us
    select_n x1, other arithmetic, on_device(): jnp.take(value_cache, page_table, axis=0)  2.67 us
  transfers between devices with their start and end apart: 1, of which 0 were waited for; matrix products, arithmetic and copies ran while one was open for 12% of the time, Pallas kernels for 0%

commit v1 on v0

v1 whole, which is shorter than its diff:
```python
import jax
import jax.numpy as jnp
from jax import lax
from jax.experimental import pallas as pl
from jax.experimental.pallas import tpu as pltpu
from jax.sharding import Mesh
from jax.sharding import PartitionSpec as P

HEADS = 32
KVH = 16
HD = 128
QSCALAR = 144
SEQ = ("seq_0", "seq_1")
FLOOR = -1e30
CHUNKS = 4


def by_request(row, values):
    request = row & 3
    picked = jnp.where(request == 0, values[0], values[1])
    return jnp.where(request >= 2, jnp.where(request == 2, values[2], values[3]), picked)


def attend_pages(meta, q_ref, k_far, v_far, out_ref, k_ref, v_ref, arrived):
    row = lax.broadcasted_iota(jnp.int32, (8, HD), 0)
    lane = lax.broadcasted_iota(jnp.int32, (8, HD), 1)
    request = row & 3
    slots = [meta[r] for r in range(4)]
    live = (lane < by_request(row, [meta[4 + r] for r in range(4)])) & (
        lane >= by_request(row, [meta[8 + r] for r in range(4)])
    )
    width = KVH * HD // CHUNKS
    loads = []
    for i, (far, near) in enumerate(((k_far, k_ref), (v_far, v_ref))):
        for c in range(CHUNKS):
            part = (slice(None), slice(None), pl.ds(c * width, width))
            loads.append(
                pltpu.make_async_copy(far.at[part], near.at[part], arrived.at[i * CHUNKS + c])
            )
    for load in loads:
        load.start()
    queries = q_ref[...].astype(jnp.float32)

    def apart(x):
        return jnp.concatenate(
            [jnp.where(request == r, x, 0.0) for r in range(4)], axis=1
        ).astype(jnp.bfloat16)

    spread, stats = [], []
    for k in range(KVH):
        if k % (KVH // CHUNKS) == 0:
            loads[k // (KVH // CHUNKS)].wait()
        keys = jnp.concatenate([k_ref[slots[r], :, k * HD : (k + 1) * HD] for r in range(4)], axis=1)
        scores = lax.dot_general(
            apart(queries[8 * k : 8 * k + 8]),
            keys,
            (((1,), (1,)), ((), ())),
            preferred_element_type=jnp.float32,
        ) * (QSCALAR ** (-0.5))
        peak = jnp.max(jnp.where(live, scores, FLOOR), axis=1, keepdims=True)
        mark = peak.astype(jnp.bfloat16).astype(jnp.float32)
        weights = jnp.where(live, jnp.exp(scores - mark), 0.0)
        total = jnp.sum(weights, axis=1, keepdims=True)
        coarse = total.astype(jnp.bfloat16).astype(jnp.float32)
        spread.append(apart(weights))
        stats.append(jnp.where(lane == 0, mark, jnp.where(lane == 1, coarse, total - coarse)))
    for k in range(KVH):
        if k % (KVH // CHUNKS) == 0:
            loads[CHUNKS + k // (KVH // CHUNKS)].wait()
        values = jnp.concatenate(
            [v_ref[slots[r], :, k * HD : (k + 1) * HD] for r in range(4)], axis=0
        )
        sums = jnp.dot(spread[k], values, preferred_element_type=jnp.float32)
        even = jnp.where(row < 4, sums, pltpu.roll(stats[k], 4, 0))
        odd = jnp.where(row < 4, pltpu.roll(sums, 4, 0), stats[k])
        out_ref[2 * k] = even.astype(jnp.bfloat16)
        out_ref[2 * k + 1] = odd.astype(jnp.bfloat16)


def merge_blocks(blocks_ref, new_score_ref, new_value_ref, out_ref):
    blocks = blocks_ref[...].astype(jnp.float32)
    sums = blocks[:, 0:4, :]
    mark = blocks[:, 4:8, 0:1]
    total = blocks[:, 4:8, 1:2] + blocks[:, 4:8, 2:3]
    new_score = new_score_ref[...]
    top = jnp.maximum(jnp.max(mark, axis=0), new_score)
    factor = jnp.exp(mark - top[None])
    own = jnp.exp(new_score - top)
    denominator = jnp.sum(total * factor, axis=0) + own
    numerator = jnp.sum(sums * factor, axis=0) + own * new_value_ref[...]
    attention = (numerator / denominator).astype(jnp.bfloat16)
    out_ref[...] = jnp.broadcast_to(attention[None], out_ref.shape)


def on_device(
    queries, key_cache, value_cache, new_key, new_value, page_table, counts, offsets, w_out
):
    requests = queries.shape[0]
    place = lax.axis_index(SEQ)
    peers = lax.axis_size(SEQ)
    groups = lax.axis_size("batch")
    page_len = key_cache.shape[1]
    vmem = pl.BlockSpec(memory_space=pltpu.VMEM)
    smem = pl.BlockSpec(memory_space=pltpu.SMEM)
    hbm = pl.BlockSpec(memory_space=pltpu.HBM)

    def near(x):
        return pltpu.with_memory_space_constraint(x, pltpu.VMEM)

    def far(x):
        return pltpu.with_memory_space_constraint(x, pltpu.HBM)

    all_queries = lax.all_to_all(
        jnp.broadcast_to(queries[None], (peers, *queries.shape)), SEQ, 0, 0, tiled=True
    )
    meta = jnp.concatenate([page_table[:, 0], counts[:, 0], offsets - place * page_len])
    column = (place // (HEADS // KVH)) * HD
    own_key = lax.dynamic_slice_in_dim(new_key, column, HD, 1).astype(jnp.float32)
    own_value = lax.dynamic_slice_in_dim(new_value, column, HD, 1).astype(jnp.float32)
    new_score = jnp.sum(queries.astype(jnp.float32) * own_key, axis=1, keepdims=True) * (
        QSCALAR ** (-0.5)
    )

    blocks = pl.pallas_call(
        attend_pages,
        out_shape=pltpu.VMEM((HEADS, 8, HD), jnp.bfloat16),
        in_specs=[smem, vmem, hbm, hbm],
        out_specs=vmem,
        scratch_shapes=[
            pltpu.VMEM(key_cache.shape, key_cache.dtype),
            pltpu.VMEM(value_cache.shape, value_cache.dtype),
            pltpu.SemaphoreType.DMA((2 * CHUNKS,)),
        ],
        compiler_params=pltpu.CompilerParams(vmem_limit_bytes=16 << 20),
    )(meta, near(all_queries.reshape(HEADS * requests, HD)), far(key_cache), far(value_cache))
    blocks = lax.all_to_all(blocks, SEQ, 0, 0, tiled=True)
    attention = pl.pallas_call(
        merge_blocks,
        out_shape=pltpu.VMEM((groups, requests, HD), jnp.bfloat16),
        in_specs=[vmem, vmem, vmem],
        out_specs=vmem,
        compiler_params=pltpu.CompilerParams(vmem_limit_bytes=16 << 20),
    )(near(blocks), near(new_score), near(own_value))
    attention = lax.all_to_all(attention, "batch", 0, 0, tiled=True)
    partial = jnp.dot(
        attention.reshape(groups * requests, HD), w_out, preferred_element_type=jnp.float32
    )
    partial = partial.reshape(peers, -1, partial.shape[1])
    partial = lax.all_to_all(partial, SEQ, 0, 0, tiled=True)
    return jnp.sum(partial, axis=0).astype(jnp.bfloat16)


def solution(mesh):
    torus = Mesh(mesh.devices.reshape(4, 8, mesh.shape["batch"]), ("seq_0", "seq_1", "batch"))
    in_specs = (
        P("batch", SEQ),
        P("batch", SEQ, None),
        P("batch", SEQ, None),
        P("batch", None),
        P("batch", None),
        P("batch", SEQ),
        P("batch", SEQ),
        P("batch"),
        P(SEQ, "batch"),
    )
    return jax.shard_map(
        on_device, mesh=torus, in_specs=in_specs, out_specs=P(SEQ, "batch"), check_vma=False
    )
```

time: 111 us -> 72.3 us (0.65)
  blocking collectives: 74.7 us -> 32.7 us
  waiting for transfers between devices: 0.01 us -> 14.6 us
  local copies, waits for them, and re-layouts: 13.3 us -> 1.5 us
  matrix products: 5.52 us -> 0.15 us
  Pallas kernels: 0 us -> 5.04 us
  starting transfers between devices: 10.5 us -> 14.4 us
  other arithmetic: 5.79 us -> 3.52 us
    all_gather x2 -> x0, blocking collectives: 30.6 us -> none  [all_in_one(): both, at, found = (lax.all_gather(jnp.concatenate(lines), axis), 0, {})]
    all_to_all x1 -> x2, waiting for transfers between devices: 0.01 us -> 14.6 us  [the longest x1 8.07 us: on_device(): blocks = lax.all_to_all(blocks, SEQ, 0, 0, tiled=True)]
    all_to_all x2, blocking collectives: 44.1 us -> 32.7 us  [the longest x1 20.7 us: on_device(): attention = lax.all_to_all(attention, 'batch', 0, 0, tiled=True)]
    gather x2 -> x0, local copies, waits for them, and re-layouts: 5.61 us -> none  [the longest x1 3.63 us: on_device(): jnp.take(value_cache, page_table, axis=0)]
    dot_general x4 -> x1, matrix products: 5.52 us -> 0.15 us  [on_device(): jnp.dot(attention.reshape(groups * requests, HD), w_out, preferred_elemen...]
    pallas_call x0 -> x2, Pallas kernels: none -> 5.04 us  [the longest x1 4.83 us: on_device(): pl.pallas_call(attend_pages, out_shape=pltpu.VMEM((HEADS, 8, HD), jnp.bfl...]
    unnamed x17 -> x2, local copies, waits for them, and re-layouts: 4.03 us -> 0.01 us
    all_to_all x1 -> x2, starting transfers between devices: 10.5 us -> 14.4 us  [the longest x1 10.5 us: on_device(): lax.all_to_all(jnp.broadcast_to(queries[None], (peers, *queries.shape)),...]
  transfers between devices with their start and end apart: 1 -> 2, of which waited for: 0 -> 2; matrix products, arithmetic and copies ran while one was open for 12% -> 4% of each run, Pallas kernels for 0% -> 0%
where the time goes in v1:
time: 72.3 us; the launch traced here: 71.9 us
  blocking collectives  32.7 us (45%)
  waiting for transfers between devices  14.6 us (20%)
  starting transfers between devices  14.4 us (20%)
  Pallas kernels  5.04 us (7%)
  other arithmetic  3.52 us (5%)
  local copies, waits for them, and re-layouts  1.5 us (2%)
    all_to_all x1, blocking collectives, on_device(): attention = lax.all_to_all(attention, 'batch', 0, 0, tiled=True)  20.7 us
    all_to_all x1, blocking collectives, on_device(): partial = lax.all_to_all(partial, SEQ, 0, 0, tiled=True)  12 us
    all_to_all x1, starting transfers between devices, on_device(): lax.all_to_all(jnp.broadcast_to(queries[None], (peers, *queries.shape)),...  10.5 us
    all_to_all x1, waiting for transfers between devices, on_device(): blocks = lax.all_to_all(blocks, SEQ, 0, 0, tiled=True)  8.07 us
    all_to_all x1, waiting for transfers between devices, on_device(): lax.all_to_all(jnp.broadcast_to(queries[None], (peers, *queries.shape)),...  6.53 us
    pallas_call x1, Pallas kernels, on_device(): pl.pallas_call(attend_pages, out_shape=pltpu.VMEM((HEADS, 8, HD), jnp.bfl...  4.83 us
    all_to_all x1, starting transfers between devices, on_device(): blocks = lax.all_to_all(blocks, SEQ, 0, 0, tiled=True)  3.86 us
  transfers between devices with their start and end apart: 2, of which 2 were waited for; matrix products, arithmetic and copies ran while one was open for 4% of the time, Pallas kernels for 0%

profile of v1, /device:TPU:1, one launch (start us, length us, event | category | flops | bytes accessed | tf_op | source)
XLA Modules:
  0.0 71.9 jit_solution(15508202652829235755)
XLA Ops:
  0.0 0.0 copy-start
  0.0 1.3 %broadcast_in_dim.2 = bf16[32,4,128]{2,1,0:T(4,128)(2,1)} broadcast(bf16[4,128]{1,0:T(4,128)(2,1)} %param.9), dimensions={1,2} | broadcast | bytes 33792 | tf_op jit(solution)/shard_map/broadcast_in_dim | solution.py:114
  1.3 10.5 %all-to-all-start = ((bf16[32,4,128]{2,1,0:T(4,128)(2,1)}), bf16[32,4,128]{2,1,0:T(4,128)(2,1)S(1)}, u32[]{:S(2)}, u32[]{:S(2)}) async-start(bf16[32,4,128]{2,1,0:T(4,128)(2,1)} %broadcast_in_dim.2), calls=%async_computation | async-start | bytes 65536 | tf_op jit(solution)/shard_map/all_to_all | solution.py:113
  11.8 0.7 broadcast_subtract_fusion
  12.5 0.8 %multiply_reduce_fusion = f32[4]{0:T(128)S(1)} fusion(bf16[4,128]{1,0:T(4,128)(2,1)} %param.9, bf16[4,2048]{1,0:T(4,128)(2,1)} %param.12, s32[]{:T(128)S(6)} %select_n.10), kind=kLoop, calls=%fused_computation.3 | loop fusion | flops 2044 | bytes 2068 | tf_op jit(solution)/shard_map/reduce_sum | solution.py:120
  13.3 0.7 %pad_add_fusion.meta = s32[12]{0:T(128)S(1)} fusion(s32[4]{0:T(128)S(1)} %broadcast_subtract_fusion, s32[4]{0:T(128)} %bitcast.11, s32[4]{0:T(128)} %bitcast.12), kind=kLoop, calls=%fused_computation.5 | loop fusion | flops 24 | bytes 96 | tf_op jit(solution)/shard_map/concatenate | solution.py:116
  14.1 6.5 %all-to-all-done = bf16[32,4,128]{2,1,0:T(4,128)(2,1)S(1)} async-done(((bf16[32,4,128]{2,1,0:T(4,128)(2,1)}), bf16[32,4,128]{2,1,0:T(4,128)(2,1)S(1)}, u32[]{:S(2)}, u32[]{:S(2)}) %all-to-all-start) | async-done | bytes 32800 | tf_op jit(solution)/shard_map/all_to_all | solution.py:113
  20.6 4.8 %shard_map.91 = bf16[32,8,128]{2,1,0:T(8,128)(2,1)} custom-call(s32[12]{0:T(128)S(1)} %pad_add_fusion.meta, bf16[128,128]{1,0:T(8,128)(2,1)S(1)} %bitcast.9, bf16[4,128,2048]{2,1,0:T(8,128)(2,1)} %k_far.1, bf16[4,128,2048]{2,1,0:T(8,128)(2,1)} %v_far.1), custom_call_target="tpu_custom_call" | custom-call | tf_op jit(solution)/shard_map/pallas_call | solution.py:124
  25.4 3.9 %all-to-all-start.1 = ((bf16[32,8,128]{2,1,0:T(8,128)(2,1)}), bf16[32,8,128]{2,1,0:T(8,128)(2,1)S(1)}, u32[]{:S(2)}, u32[]{:S(2)}) async-start(bf16[32,8,128]{2,1,0:T(8,128)(2,1)} %shard_map.91), calls=%async_computation.1 | async-start | bytes 131072 | tf_op jit(solution)/shard_map/all_to_all | solution.py:136
  29.3 0.1 copy.12.new_score_ref
  29.4 0.7 dynamic-slice_convert_fusion.new_value_ref
  30.1 8.1 %all-to-all-done.1.blocks_ref = bf16[32,8,128]{2,1,0:T(8,128)(2,1)S(1)} async-done(((bf16[32,8,128]{2,1,0:T(8,128)(2,1)}), bf16[32,8,128]{2,1,0:T(8,128)(2,1)S(1)}, u32[]{:S(2)}, u32[]{:S(2)}) %all-to-all-start.1) | async-done | bytes 65568 | tf_op jit(solution)/shard_map/all_to_all | solution.py:136
  38.2 0.2 shard_map.92
  38.4 20.7 %all_to_all.20 = bf16[16,4,128]{2,1,0:T(4,128)(2,1)S(1)} all-to-all(bf16[16,4,128]{2,1,0:T(4,128)(2,1)S(1)} %shard_map.92), channel_id=1, replica_groups=mesh['seq_0'=4,'seq_1'=8,'batch'=16] {'batch'}, dimensions={0} | all-to-all | bytes 32768 | tf_op jit(solution)/shard_map/all_to_all | solution.py:144
  59.1 0.0 copy-done
  59.1 0.2 fusion
  59.2 0.1 copy.14
  59.3 12.0 %all_to_all.21 = f32[32,2,288]{2,1,0:T(2,128)S(1)} all-to-all(f32[32,2,288]{2,1,0:T(2,128)S(1)} %copy.14), channel_id=1, replica_groups=mesh['seq_0'=4,'seq_1'=8,'batch'=16] {'seq_0','seq_1'}, dimensions={0} | all-to-all | bytes 147456 | tf_op jit(solution)/shard_map/all_to_all | solution.py:149
  71.3 0.6 reduce_sum.19
  (1 shorter events, 0.0 us)
Async XLA Ops:
  0.0 59.1 %copy-start = (bf16[128,288]{0,1:T(8,128)(2,1)S(1)}, bf16[128,288]{0,1:T(8,128)(2,1)}, u32[]{:S(2)}) copy-start(bf16[128,288]{0,1:T(8,128)(2,1)} %param.17) | copy-start | bytes 221188
  1.3 19.3 %all-to-all-start = ((bf16[32,4,128]{2,1,0:T(4,128)(2,1)}), bf16[32,4,128]{2,1,0:T(4,128)(2,1)S(1)}, u32[]{:S(2)}, u32[]{:S(2)}) async-start(bf16[32,4,128]{2,1,0:T(4,128)(2,1)} %broadcast_in_dim.2), calls=%async_computation | async-start | bytes 65536 | tf_op jit(solution)/shard_map/all_to_all | solution.py:113
  25.4 12.7 %all-to-all-start.1 = ((bf16[32,8,128]{2,1,0:T(8,128)(2,1)}), bf16[32,8,128]{2,1,0:T(8,128)(2,1)S(1)}, u32[]{:S(2)}, u32[]{:S(2)}) async-start(bf16[32,8,128]{2,1,0:T(8,128)(2,1)} %shard_map.91), calls=%async_computation.1 | async-start | bytes 131072 | tf_op jit(solution)/shard_map/all_to_all | solution.py:136

commit v2 on v1

v2 whole, which is shorter than its diff:
```python
import jax
import jax.numpy as jnp
from jax import lax
from jax.experimental import pallas as pl
from jax.experimental.pallas import tpu as pltpu
from jax.sharding import Mesh
from jax.sharding import PartitionSpec as P

HEADS = 32
KVH = 16
HD = 128
QSCALAR = 144
SCALE = QSCALAR ** (-0.5)
SEQ = ("seq_0", "seq_1")
FLOOR = -1e30
LOADS = 12


def by_request(row, values):
    request = row & 3
    picked = jnp.where(request == 0, values[0], values[1])
    return jnp.where(request >= 2, jnp.where(request == 2, values[2], values[3]), picked)


def fetch_pages(
    place_ref, table_ref, counts_ref, offsets_ref, q_ref, new_key_ref, new_value_ref,
    k_far, v_far, k_ref, v_ref, later_ref, limits_ref, own_ref, arrived,
):
    half = v_ref.shape[2]
    loads = []
    for r in range(4):
        slot = table_ref[r]
        for source, target in (
            (k_far.at[slot], k_ref.at[r]),
            (v_far.at[slot, :, pl.ds(0, half)], v_ref.at[r]),
            (v_far.at[slot, :, pl.ds(half, half)], later_ref.at[r]),
        ):
            loads.append(pltpu.make_async_copy(source, target, arrived.at[len(loads)]))
    for load in loads:
        load.start()
    place = place_ref[0]
    row = lax.broadcasted_iota(jnp.int32, (8, HD), 0)
    limits_ref[0:8] = by_request(row, [counts_ref[r] for r in range(4)])
    limits_ref[8:16] = by_request(row, [offsets_ref[r] - place * HD for r in range(4)])
    column = pl.multiple_of((place // (HEADS // KVH)) * HD, HD)
    key = new_key_ref[:, pl.ds(column, HD)].astype(jnp.float32)
    score = jnp.sum(q_ref[...].astype(jnp.float32) * key, axis=1, keepdims=True) * SCALE
    own_ref[0:4] = jnp.broadcast_to(score, (4, HD))
    own_ref[4:8] = new_value_ref[:, pl.ds(column, HD)].astype(jnp.float32)
    for load in loads:
        load.wait()


def attend_pages(q_ref, k_ref, v_ref, later_far, limits_ref, out_ref, later_ref, arrived):
    later = pltpu.make_async_copy(later_far, later_ref, arrived)
    later.start()
    row = lax.broadcasted_iota(jnp.int32, (8, HD), 0)
    lane = lax.broadcasted_iota(jnp.int32, (8, HD), 1)
    request = row & 3
    live = (lane < limits_ref[0:8]) & (lane >= limits_ref[8:16])
    queries = q_ref[...].astype(jnp.float32)

    def apart(x):
        return jnp.concatenate(
            [jnp.where(request == r, x, 0.0) for r in range(4)], axis=1
        ).astype(jnp.bfloat16)

    for k in range(KVH):
        cols = slice(k * HD, (k + 1) * HD)
        keys = jnp.concatenate([k_ref[r, :, cols] for r in range(4)], axis=1)
        scores = lax.dot_general(
            apart(queries[8 * k : 8 * k + 8]),
            keys,
            (((1,), (1,)), ((), ())),
            preferred_element_type=jnp.float32,
        ) * SCALE
        peak = jnp.max(jnp.where(live, scores, FLOOR), axis=1, keepdims=True)
        weights = jnp.where(live, jnp.exp(scores - peak), 0.0)
        if k == KVH // 2:
            later.wait()
        held = v_ref if k < KVH // 2 else later_ref
        cols = slice(k % (KVH // 2) * HD, (k % (KVH // 2) + 1) * HD)
        values = jnp.concatenate([held[r, :, cols] for r in range(4)], axis=0)
        sums = jnp.dot(apart(weights), values, preferred_element_type=jnp.float32)
        mark = peak.astype(jnp.bfloat16).astype(jnp.float32)
        shift = jnp.exp(jnp.minimum(peak - mark, 64.0))
        total = jnp.sum(weights, axis=1, keepdims=True) * shift
        coarse = total.astype(jnp.bfloat16).astype(jnp.float32)
        sums = sums * shift
        stats = jnp.where(lane == 0, mark, jnp.where(lane == 1, coarse, total - coarse))
        even = jnp.where(row < 4, sums, pltpu.roll(stats, 4, 0))
        odd = jnp.where(row < 4, pltpu.roll(sums, 4, 0), stats)
        out_ref[2 * k] = even.astype(jnp.bfloat16)
        out_ref[2 * k + 1] = odd.astype(jnp.bfloat16)


def merge_blocks(blocks_ref, own_ref, out_ref):
    blocks = blocks_ref[...].astype(jnp.float32)
    sums = blocks[:, 0:4, :]
    mark = blocks[:, 4:8, 0:1]
    total = blocks[:, 4:8, 1:2] + blocks[:, 4:8, 2:3]
    new_score = own_ref[0:4, 0:1]
    top = jnp.maximum(jnp.max(mark, axis=0), new_score)
    factor = jnp.exp(mark - top[None])
    own = jnp.exp(new_score - top)
    denominator = jnp.sum(total * factor, axis=0) + own
    numerator = jnp.sum(sums * factor, axis=0) + own * own_ref[4:8]
    attention = (numerator / denominator).astype(jnp.bfloat16)
    out_ref[...] = jnp.broadcast_to(attention[None], out_ref.shape)


def on_device(
    queries, key_cache, value_cache, new_key, new_value, page_table, counts, offsets, w_out
):
    requests = queries.shape[0]
    place = lax.axis_index(SEQ)
    peers = lax.axis_size(SEQ)
    groups = lax.axis_size("batch")
    vmem = pl.BlockSpec(memory_space=pltpu.VMEM)
    smem = pl.BlockSpec(memory_space=pltpu.SMEM)
    hbm = pl.BlockSpec(memory_space=pltpu.HBM)
    half = (*value_cache.shape[:2], value_cache.shape[2] // 2)
    small = pltpu.CompilerParams(vmem_limit_bytes=8 << 20)

    def near(x):
        return pltpu.with_memory_space_constraint(x, pltpu.VMEM)

    def far(x):
        return pltpu.with_memory_space_constraint(x, pltpu.HBM)

    all_queries = lax.all_to_all(
        jnp.broadcast_to(queries[None], (peers, *queries.shape)), SEQ, 0, 0, tiled=True
    )
    keys, values, later, limits, own = pl.pallas_call(
        fetch_pages,
        out_shape=(
            pltpu.VMEM(key_cache.shape, key_cache.dtype),
            pltpu.VMEM(half, value_cache.dtype),
            pltpu.HBM(half, value_cache.dtype),
            pltpu.VMEM((16, HD), jnp.int32),
            pltpu.VMEM((8, HD), jnp.float32),
        ),
        in_specs=[smem] * 4 + [vmem] * 3 + [hbm] * 2,
        out_specs=(vmem, vmem, hbm, vmem, vmem),
        scratch_shapes=[pltpu.SemaphoreType.DMA((LOADS,))],
        compiler_params=small,
    )(
        place.reshape(1), page_table[:, 0], counts[:, 0], offsets,
        queries, new_key, new_value, far(key_cache), far(value_cache),
    )
    blocks = pl.pallas_call(
        attend_pages,
        out_shape=pltpu.VMEM((HEADS, 8, HD), jnp.bfloat16),
        in_specs=[vmem, vmem, vmem, hbm, vmem],
        out_specs=vmem,
        scratch_shapes=[pltpu.VMEM(half, value_cache.dtype), pltpu.SemaphoreType.DMA],
        compiler_params=small,
    )(near(all_queries.reshape(HEADS * requests, HD)), near(keys), near(values), far(later), near(limits))
    blocks = lax.all_to_all(blocks, SEQ, 0, 0, tiled=True)
    attention = pl.pallas_call(
        merge_blocks,
        out_shape=pltpu.VMEM((groups, requests, HD), jnp.bfloat16),
        in_specs=[vmem] * 2,
        out_specs=vmem,
        compiler_params=small,
    )(near(blocks), near(own))
    attention = lax.all_to_all(attention, "batch", 0, 0, tiled=True)
    partial = jnp.dot(
        attention.reshape(groups * requests, HD), w_out, preferred_element_type=jnp.float32
    )
    partial = partial.reshape(peers, -1, partial.shape[1])
    partial = lax.all_to_all(partial, SEQ, 0, 0, tiled=True)
    return jnp.sum(partial, axis=0).astype(jnp.bfloat16)


def solution(mesh):
    torus = Mesh(mesh.devices.reshape(4, 8, mesh.shape["batch"]), ("seq_0", "seq_1", "batch"))
    in_specs = (
        P("batch", SEQ),
        P("batch", SEQ, None),
        P("batch", SEQ, None),
        P("batch", None),
        P("batch", None),
        P("batch", SEQ),
        P("batch", SEQ),
        P("batch"),
        P(SEQ, "batch"),
    )
    return jax.shard_map(
        on_device, mesh=torus, in_specs=in_specs, out_specs=P(SEQ, "batch"), check_vma=False
    )
```

time: 72.3 us -> 106 us (1.47)
  Pallas kernels: 5.04 us -> 38.5 us
  blocking collectives: 32.7 us -> 50 us
  waiting for transfers between devices: 14.6 us -> 0.01 us
  local copies, waits for them, and re-layouts: 1.5 us -> 5.47 us
  starting transfers between devices: 14.4 us -> 10.5 us
  other arithmetic: 3.52 us -> 0.61 us
    pallas_call x0 -> x1, Pallas kernels: none -> 33.5 us  [on_device(): pl.pallas_call(fetch_pages, out_shape=(pltpu.VMEM(key_cache.shape, key_ca...]
    all_to_all x0 -> x1, blocking collectives: none -> 18 us  [on_device(): blocks = lax.all_to_all(blocks, SEQ, 0, 0, tiled=True)]
    all_to_all x1 -> x0, waiting for transfers between devices: 8.07 us -> none  [on_device(): blocks = lax.all_to_all(blocks, SEQ, 0, 0, tiled=True)]
    all_to_all x1, waiting for transfers between devices: 6.53 us -> 0.01 us  [on_device(): lax.all_to_all(jnp.broadcast_to(queries[None], (peers, *queries.shape)),...]
    unnamed x2 -> x14, local copies, waits for them, and re-layouts: 0.01 us -> 4.08 us
    all_to_all x1 -> x0, starting transfers between devices: 3.86 us -> none  [on_device(): blocks = lax.all_to_all(blocks, SEQ, 0, 0, tiled=True)]
  transfers between devices with their start and end apart: 2 -> 1, of which waited for: 2 -> 0; matrix products, arithmetic and copies ran while one was open for 4% -> 0% of each run, Pallas kernels for 0% -> 32%
where the time goes in v2:
time: 106 us; the launch traced here: 105 us
  blocking collectives  50 us (47%)
  Pallas kernels  38.5 us (36%)
  starting transfers between devices  10.5 us (10%)
  local copies, waits for them, and re-layouts  5.47 us (5%)
    pallas_call x1, Pallas kernels, on_device(): pl.pallas_call(fetch_pages, out_shape=(pltpu.VMEM(key_cache.shape, key_ca...  33.5 us
    all_to_all x1, blocking collectives, on_device(): attention = lax.all_to_all(attention, 'batch', 0, 0, tiled=True)  20 us
    all_to_all x1, blocking collectives, on_device(): blocks = lax.all_to_all(blocks, SEQ, 0, 0, tiled=True)  18 us
    all_to_all x1, blocking collectives, on_device(): partial = lax.all_to_all(partial, SEQ, 0, 0, tiled=True)  12 us
    all_to_all x1, starting transfers between devices, on_device(): lax.all_to_all(jnp.broadcast_to(queries[None], (peers, *queries.shape)),...  10.5 us
    pallas_call x1, Pallas kernels, on_device(): pl.pallas_call(attend_pages, out_shape=pltpu.VMEM((HEADS, 8, HD), jnp.bfl...  4.73 us
    unnamed x14, local copies, waits for them, and re-layouts  4.08 us
  transfers between devices with their start and end apart: 1, of which 0 were waited for; matrix products, arithmetic and copies ran while one was open for 0% of the time, Pallas kernels for 32%

profile of v2, /device:TPU:1, one launch (start us, length us, event | category | flops | bytes accessed | tf_op | source)
XLA Modules:
  0.0 105.3 jit_solution(16577343946733894918)
XLA Ops:
  0.0 0.0 copy-start
  0.0 1.3 %broadcast_in_dim.2 = bf16[32,4,128]{2,1,0:T(4,128)(2,1)} broadcast(bf16[4,128]{1,0:T(4,128)(2,1)} %q_ref.1), dimensions={1,2} | broadcast | bytes 33792 | tf_op jit(solution)/shard_map/broadcast_in_dim | solution.py:132
  1.3 10.5 %all-to-all-start = ((bf16[32,4,128]{2,1,0:T(4,128)(2,1)}), bf16[32,4,128]{2,1,0:T(4,128)(2,1)S(1)}, u32[]{:S(2)}, u32[]{:S(2)}) async-start(bf16[32,4,128]{2,1,0:T(4,128)(2,1)} %broadcast_in_dim.2), calls=%async_computation | async-start | bytes 65536 | tf_op jit(solution)/shard_map/all_to_all | solution.py:131
  11.8 0.0 copy-start.1
  11.8 0.7 copy-done.1
  12.5 0.0 copy-start.2
  12.5 0.7 copy-done.2
  13.3 0.0 copy-start.3
  13.3 0.7 copy-done.3
  13.9 0.0 copy-start.4
  13.9 0.7 copy-done.4
  14.6 0.0 copy-start.5
  14.6 0.7 copy-done.5
  15.3 0.0 copy-start.6
  15.3 0.7 copy-done.6
  15.9 33.5 %shard_map.91 = (bf16[4,128,2048]{2,1,0:T(8,128)(2,1)S(1)}, bf16[4,128,1024]{2,1,0:T(8,128)(2,1)S(1)}, bf16[4,128,1024]{2,1,0:T(8,128)(2,1)}, s32[16,128]{1,0:T(8,128)S(1)}, f32[8,128]{1,0:T(8,128)S(1)}) custom-call(s32[1]{0:T(128)} %bitcast.1.place_ref, s32[4]{0:T(128)S(1)} %bitcast.9, s32[4]{0:T(128)S(1)} %bitcast.10, s32[4]{0:T(128)S(1)} %copy-done.6, ...), custom_call_target="tpu_custom_call" | custom-call | tf_op jit(solution)/shard_map/pallas_call | solution.py:134
  49.4 0.0 all-to-all-done
  49.5 4.7 %shard_map.92 = bf16[32,8,128]{2,1,0:T(8,128)(2,1)S(1)} custom-call(bf16[128,128]{1,0:T(8,128)(2,1)S(1)} %bitcast.8, bf16[4,128,2048]{2,1,0:T(8,128)(2,1)S(1)} %get-tuple-element.10.k_ref, bf16[4,128,1024]{2,1,0:T(8,128)(2,1)S(1)} %get-tuple-element.11.v_ref, bf16[4,128,1024]{2,1,0:T(8,128)(2,1)} %get-tuple-element.12.later_far, ...), custom_call_target="tpu_custom_call" | custom-call | tf_op jit(solution)/shard_map/pallas_call | solution.py:151
  54.2 18.0 %all_to_all.20.blocks_ref = bf16[32,8,128]{2,1,0:T(8,128)(2,1)S(1)} all-to-all(bf16[32,8,128]{2,1,0:T(8,128)(2,1)S(1)} %shard_map.92), channel_id=1, replica_groups=mesh['seq_0'=4,'seq_1'=8,'batch'=16] {'seq_0','seq_1'}, dimensions={0} | all-to-all | bytes 131072 | tf_op jit(solution)/shard_map/all_to_all | solution.py:159
  72.2 0.2 shard_map.93
  72.4 20.0 %all_to_all.21 = bf16[16,4,128]{2,1,0:T(4,128)(2,1)S(1)} all-to-all(bf16[16,4,128]{2,1,0:T(4,128)(2,1)S(1)} %shard_map.93), channel_id=1, replica_groups=mesh['seq_0'=4,'seq_1'=8,'batch'=16] {'batch'}, dimensions={0} | all-to-all | bytes 32768 | tf_op jit(solution)/shard_map/all_to_all | solution.py:167
  92.4 0.0 copy-done
  92.4 0.2 fusion
  92.6 0.1 copy.12
  92.7 12.0 %all_to_all.22 = f32[32,2,288]{2,1,0:T(2,128)S(1)} all-to-all(f32[32,2,288]{2,1,0:T(2,128)S(1)} %copy.12), channel_id=1, replica_groups=mesh['seq_0'=4,'seq_1'=8,'batch'=16] {'seq_0','seq_1'}, dimensions={0} | all-to-all | bytes 147456 | tf_op jit(solution)/shard_map/all_to_all | solution.py:172
  104.7 0.6 reduce_sum.9
Async XLA Ops:
  0.0 92.4 %copy-start = (bf16[128,288]{0,1:T(8,128)(2,1)S(1)}, bf16[128,288]{0,1:T(8,128)(2,1)}, u32[]{:S(2)}) copy-start(bf16[128,288]{0,1:T(8,128)(2,1)} %param.17) | copy-start | bytes 221188
  1.3 48.1 %all-to-all-start = ((bf16[32,4,128]{2,1,0:T(4,128)(2,1)}), bf16[32,4,128]{2,1,0:T(4,128)(2,1)S(1)}, u32[]{:S(2)}, u32[]{:S(2)}) async-start(bf16[32,4,128]{2,1,0:T(4,128)(2,1)} %broadcast_in_dim.2), calls=%async_computation | async-start | bytes 65536 | tf_op jit(solution)/shard_map/all_to_all | solution.py:131
  11.8 0.7 copy-start.1
  12.5 0.7 copy-start.2
  13.3 0.7 copy-start.3
  13.9 0.7 copy-start.4
  14.6 0.7 copy-start.5
  15.3 0.7 copy-start.6

commit v3 on v2

v3 whole, which is shorter than its diff:
```python
import jax
import jax.numpy as jnp
from jax import lax
from jax.experimental import pallas as pl
from jax.experimental.pallas import tpu as pltpu
from jax.sharding import Mesh
from jax.sharding import PartitionSpec as P

HEADS = 32
KVH = 16
HD = 128
QSCALAR = 144
SCALE = QSCALAR ** (-0.5)
SEQ = ("seq_0", "seq_1")
FLOOR = -1e30
UNROLL = 4


def by_request(row, values):
    request = row & 3
    picked = jnp.where(request == 0, values[0], values[1])
    return jnp.where(request >= 2, jnp.where(request == 2, values[2], values[3]), picked)


def fetch_pages(
    table_far, counts_far, offsets_far, q_far, new_key_far, new_value_far, k_far, v_far,
    k_ref, v_ref, rows_ref, own_ref,
    table_ref, counts_ref, offsets_ref, q_ref, new_key_ref, new_value_ref, arrived,
):
    place = lax.axis_index(SEQ)
    column = pl.multiple_of((place // (HEADS // KVH)) * HD, HD)
    half = v_ref.shape[2]
    loads = [
        pltpu.make_async_copy(source, target, arrived.at[i])
        for i, (source, target) in enumerate(
            (
                (table_far, table_ref),
                (counts_far, counts_ref),
                (offsets_far, offsets_ref),
                (q_far, q_ref),
                (new_key_far.at[:, pl.ds(column, HD)], new_key_ref),
                (new_value_far.at[:, pl.ds(column, HD)], new_value_ref),
                (k_far, k_ref),
                (v_far.at[:, :, pl.ds(0, half)], v_ref),
            )
        )
    ]
    for load in loads:
        load.start()
    row = lax.broadcasted_iota(jnp.int32, (8, HD), 0)
    for load in loads[:6]:
        load.wait()
    rows_ref[0] = by_request(row, [table_ref[r] for r in range(4)])
    rows_ref[1] = by_request(row, [counts_ref[r] for r in range(4)])
    rows_ref[2] = by_request(row, [offsets_ref[r] - place * HD for r in range(4)])
    key = new_key_ref[...].astype(jnp.float32)
    score = jnp.sum(q_ref[...].astype(jnp.float32) * key, axis=1, keepdims=True) * SCALE
    own_ref[0:4] = jnp.broadcast_to(score, (4, HD))
    own_ref[4:8] = new_value_ref[...].astype(jnp.float32)
    for load in loads[6:]:
        load.wait()


def attend_pages(
    q_ref, k_ref, v_ref, v_far, rows_ref, out_ref,
    later_ref, wide_ref, scores_ref, stats_ref, arrived,
):
    half = later_ref.shape[2]
    later = pltpu.make_async_copy(v_far.at[:, :, pl.ds(half, half)], later_ref, arrived)
    later.start()
    row = lax.broadcasted_iota(jnp.int32, (8, HD), 0)
    lane = lax.broadcasted_iota(jnp.int32, (8, HD), 1)
    slot = rows_ref[0]

    def apart(x):
        return jnp.concatenate(
            [jnp.where(slot == i, x, 0.0) for i in range(4)], axis=1
        ).astype(jnp.bfloat16)

    wide_ref[...] = q_ref[...].astype(jnp.float32)

    def score(i, carry):
        for j in range(UNROLL):
            k = i * UNROLL + j
            rows = pl.ds(pl.multiple_of(k * 8, 8), 8)
            cols = pl.ds(pl.multiple_of(k * HD, HD), HD)
            keys = jnp.concatenate([k_ref[i, :, cols] for i in range(4)], axis=1)
            scores_ref[rows] = lax.dot_general(
                apart(wide_ref[rows]),
                keys,
                (((1,), (1,)), ((), ())),
                preferred_element_type=jnp.float32,
            )
        return carry

    lax.fori_loop(0, KVH // UNROLL, score, 0)
    live = ((lane < rows_ref[1]) & (lane >= rows_ref[2]))[None]
    scores = scores_ref[...].reshape(KVH, 8, HD) * SCALE
    peak = jnp.max(jnp.where(live, scores, FLOOR), axis=2, keepdims=True)
    weights = jnp.where(live, jnp.exp(scores - peak), 0.0)
    mark = peak.astype(jnp.bfloat16).astype(jnp.float32)
    shift = jnp.exp(jnp.minimum(peak - mark, 64.0))
    total = jnp.sum(weights, axis=2, keepdims=True) * shift
    coarse = total.astype(jnp.bfloat16).astype(jnp.float32)
    stats = jnp.where(lane == 1, coarse, jnp.where(lane == 2, total - coarse, shift))
    scores_ref[...] = weights.reshape(KVH * 8, HD)
    stats_ref[...] = jnp.where(lane == 0, mark, stats).reshape(KVH * 8, HD)

    def value(held, base):
        def step(i, carry):
            for j in range(UNROLL):
                k = i * UNROLL + j
                rows = pl.ds(pl.multiple_of((base + k) * 8, 8), 8)
                cols = pl.ds(pl.multiple_of(k * HD, HD), HD)
                values = jnp.concatenate([held[i, :, cols] for i in range(4)], axis=0)
                sums = jnp.dot(
                    apart(scores_ref[rows]), values, preferred_element_type=jnp.float32
                )
                stats = stats_ref[rows]
                sums = sums * stats[:, 3:4]
                even = jnp.where(row < 4, sums, pltpu.roll(stats, 4, 0))
                odd = jnp.where(row < 4, pltpu.roll(sums, 4, 0), stats)
                out_ref[2 * (base + k)] = even.astype(jnp.bfloat16)
                out_ref[2 * (base + k) + 1] = odd.astype(jnp.bfloat16)
            return carry

        return step

    lax.fori_loop(0, KVH // 2 // UNROLL, value(v_ref, 0), 0)
    later.wait()
    lax.fori_loop(0, KVH // 2 // UNROLL, value(later_ref, KVH // 2), 0)


def merge_blocks(blocks_ref, own_ref, out_ref):
    blocks = blocks_ref[...].astype(jnp.float32)
    sums = blocks[:, 0:4, :]
    mark = blocks[:, 4:8, 0:1]
    total = blocks[:, 4:8, 1:2] + blocks[:, 4:8, 2:3]
    new_score = own_ref[0:4, 0:1]
    top = jnp.maximum(jnp.max(mark, axis=0), new_score)
    factor = jnp.exp(mark - top[None])
    own = jnp.exp(new_score - top)
    denominator = jnp.sum(total * factor, axis=0) + own
    numerator = jnp.sum(sums * factor, axis=0) + own * own_ref[4:8]
    attention = (numerator / denominator).astype(jnp.bfloat16)
    out_ref[...] = jnp.broadcast_to(attention[None], out_ref.shape)


def merged_attention(
    queries, key_cache, value_cache, new_key, new_value, page_table, counts, offsets, groups
):
    requests = queries.shape[0]
    peers = lax.axis_size(SEQ)
    vmem = pl.BlockSpec(memory_space=pltpu.VMEM)
    hbm = pl.BlockSpec(memory_space=pltpu.HBM)
    half = (*value_cache.shape[:2], value_cache.shape[2] // 2)
    small = pltpu.CompilerParams(vmem_limit_bytes=8 << 20)

    def near(x):
        return pltpu.with_memory_space_constraint(x, pltpu.VMEM)

    def far(x):
        return pltpu.with_memory_space_constraint(x, pltpu.HBM)

    all_queries = lax.all_to_all(
        jnp.broadcast_to(queries[None], (peers, *queries.shape)), SEQ, 0, 0, tiled=True
    )
    keys, values, rows, own = pl.pallas_call(
        fetch_pages,
        out_shape=(
            pltpu.VMEM(key_cache.shape, key_cache.dtype),
            pltpu.VMEM(half, value_cache.dtype),
            pltpu.VMEM((3, 8, HD), jnp.int32),
            pltpu.VMEM((8, HD), jnp.float32),
        ),
        in_specs=[hbm] * 8,
        out_specs=(vmem,) * 4,
        scratch_shapes=[pltpu.SMEM((requests,), jnp.int32)] * 3
        + [pltpu.VMEM((requests, HD), jnp.bfloat16)] * 3
        + [pltpu.SemaphoreType.DMA((8,))],
        compiler_params=small,
    )(
        far(page_table[:, 0]), far(counts[:, 0]), far(offsets),
        far(queries), far(new_key), far(new_value), far(key_cache), far(value_cache),
    )
    blocks = pl.pallas_call(
        attend_pages,
        out_shape=pltpu.VMEM((HEADS, 8, HD), jnp.bfloat16),
        in_specs=[vmem, vmem, vmem, hbm, vmem],
        out_specs=vmem,
        scratch_shapes=[pltpu.VMEM(half, value_cache.dtype)]
        + [pltpu.VMEM((HEADS * requests, HD), jnp.float32)] * 3
        + [pltpu.SemaphoreType.DMA],
        compiler_params=small,
    )(
        near(all_queries.reshape(HEADS * requests, HD)),
        near(keys), near(values), far(value_cache), near(rows),
    )
    blocks = lax.all_to_all(blocks, SEQ, 0, 0, tiled=True)
    attention = pl.pallas_call(
        merge_blocks,
        out_shape=pltpu.VMEM((groups, requests, HD), jnp.bfloat16),
        in_specs=[vmem] * 2,
        out_specs=vmem,
        compiler_params=small,
    )(near(blocks), near(own))
    return attention


def on_device(
    queries, key_cache, value_cache, new_key, new_value, page_table, counts, offsets, w_out
):
    requests = queries.shape[0]
    peers = lax.axis_size(SEQ)
    groups = lax.axis_size("batch")
    attention = merged_attention(
        queries, key_cache, value_cache, new_key, new_value, page_table, counts, offsets, groups
    )
    attention = lax.all_to_all(attention, "batch", 0, 0, tiled=True)
    partial = jnp.dot(
        attention.reshape(groups * requests, HD), w_out, preferred_element_type=jnp.float32
    )
    partial = partial.reshape(peers, -1, partial.shape[1])
    partial = lax.all_to_all(partial, SEQ, 0, 0, tiled=True)
    return jnp.sum(partial, axis=0).astype(jnp.bfloat16)


def solution(mesh):
    torus = Mesh(mesh.devices.reshape(4, 8, mesh.shape["batch"]), ("seq_0", "seq_1", "batch"))
    in_specs = (
        P("batch", SEQ),
        P("batch", SEQ, None),
        P("batch", SEQ, None),
        P("batch", None),
        P("batch", None),
        P("batch", SEQ),
        P("batch", SEQ),
        P("batch"),
        P(SEQ, "batch"),
    )
    return jax.shard_map(
        on_device, mesh=torus, in_specs=in_specs, out_specs=P(SEQ, "batch"), check_vma=False
    )
```

time: 106 us -> 68.8 us (0.65)
  Pallas kernels: 38.5 us -> 4.47 us
  waiting for transfers between devices: 0.01 us -> 6.78 us
  blocking collectives: 50 us -> 44.5 us
  local copies, waits for them, and re-layouts: 5.47 us -> 1.4 us
    pallas_call x3, Pallas kernels: 38.5 us -> 4.47 us  [the longest x1 2.27 us: merged_attention(): pl.pallas_call(attend_pages, out_shape=pltpu.VMEM((HEADS, 8, HD), jnp.bfl...]
    all_to_all x1, waiting for transfers between devices: 0.01 us -> 6.78 us  [merged_attention(): lax.all_to_all(jnp.broadcast_to(queries[None], (peers, *queries.shape)),...]
    all_to_all x1, blocking collectives: 18 us -> 11.8 us  [merged_attention(): blocks = lax.all_to_all(blocks, SEQ, 0, 0, tiled=True)]
    unnamed x14 -> x2, local copies, waits for them, and re-layouts: 4.08 us -> 0.01 us
  transfers between devices with their start and end apart: 1 -> 1, of which waited for: 0 -> 1; matrix products, arithmetic and copies ran while one was open for 0% -> 0% of each run, Pallas kernels for 32% -> 3%
where the time goes in v3:
time: 68.8 us; the launch traced here: 68.5 us
  blocking collectives  44.5 us (65%)
  starting transfers between devices  10.5 us (15%)
  waiting for transfers between devices  6.78 us (10%)
  Pallas kernels  4.47 us (6%)
  local copies, waits for them, and re-layouts  1.4 us (2%)
    all_to_all x1, blocking collectives, on_device(): attention = lax.all_to_all(attention, 'batch', 0, 0, tiled=True)  20.7 us
    all_to_all x1, blocking collectives, on_device(): partial = lax.all_to_all(partial, SEQ, 0, 0, tiled=True)  12 us
    all_to_all x1, blocking collectives, merged_attention(): blocks = lax.all_to_all(blocks, SEQ, 0, 0, tiled=True)  11.8 us
    all_to_all x1, starting transfers between devices, merged_attention(): lax.all_to_all(jnp.broadcast_to(queries[None], (peers, *queries.shape)),...  10.5 us
    all_to_all x1, waiting for transfers between devices, merged_attention(): lax.all_to_all(jnp.broadcast_to(queries[None], (peers, *queries.shape)),...  6.78 us
    pallas_call x1, Pallas kernels, merged_attention(): pl.pallas_call(attend_pages, out_shape=pltpu.VMEM((HEADS, 8, HD), jnp.bfl...  2.27 us
    pallas_call x1, Pallas kernels, merged_attention(): pl.pallas_call(fetch_pages, out_shape=(pltpu.VMEM(key_cache.shape, key_ca...  1.99 us
  transfers between devices with their start and end apart: 1, of which 1 were waited for; matrix products, arithmetic and copies ran while one was open for 0% of the time, Pallas kernels for 3%

profile of v3, /device:TPU:1, one launch (start us, length us, event | category | flops | bytes accessed | tf_op | source)
XLA Modules:
  0.0 68.5 jit_solution(1142619415615258543)
XLA Ops:
  0.0 0.0 copy-start
  0.0 1.3 %broadcast_in_dim.2 = bf16[32,4,128]{2,1,0:T(4,128)(2,1)} broadcast(bf16[4,128]{1,0:T(4,128)(2,1)} %q_far.1), dimensions={1,2} | broadcast | bytes 33792 | tf_op jit(solution)/shard_map/broadcast_in_dim | solution.py:166
  1.3 10.5 %all-to-all-start = ((bf16[32,4,128]{2,1,0:T(4,128)(2,1)}), bf16[32,4,128]{2,1,0:T(4,128)(2,1)S(1)}, u32[]{:S(2)}, u32[]{:S(2)}) async-start(bf16[32,4,128]{2,1,0:T(4,128)(2,1)} %broadcast_in_dim.2), calls=%async_computation | async-start | bytes 65536 | tf_op jit(solution)/shard_map/all_to_all | solution.py:165
  11.8 2.0 %shard_map.91 = (bf16[4,128,2048]{2,1,0:T(8,128)(2,1)S(1)}, bf16[4,128,1024]{2,1,0:T(8,128)(2,1)S(1)}, s32[3,8,128]{2,1,0:T(8,128)S(1)}, f32[8,128]{1,0:T(8,128)S(1)}) custom-call(s32[4]{0:T(128)} %bitcast.9, s32[4]{0:T(128)} %bitcast.10, s32[4]{0:T(128)} %offsets_far.1, bf16[4,128]{1,0:T(4,128)(2,1)} %q_far.1, bf16[4,2048]{1,0:T(4,128)(2,1)} %new_key_far.1, ...), custom_call_target="tpu_custom_call" | custom-call | tf_op jit(solution)/shard_map/pallas_call | solution.py:168
  13.8 6.8 %all-to-all-done = bf16[32,4,128]{2,1,0:T(4,128)(2,1)S(1)} async-done(((bf16[32,4,128]{2,1,0:T(4,128)(2,1)}), bf16[32,4,128]{2,1,0:T(4,128)(2,1)S(1)}, u32[]{:S(2)}, u32[]{:S(2)}) %all-to-all-start) | async-done | bytes 32800 | tf_op jit(solution)/shard_map/all_to_all | solution.py:165
  20.6 2.3 %shard_map.92 = bf16[32,8,128]{2,1,0:T(8,128)(2,1)S(1)} custom-call(bf16[128,128]{1,0:T(8,128)(2,1)S(1)} %bitcast.7, bf16[4,128,2048]{2,1,0:T(8,128)(2,1)S(1)} %get-tuple-element.9.k_ref, bf16[4,128,1024]{2,1,0:T(8,128)(2,1)S(1)} %get-tuple-element.10.v_ref, bf16[4,128,2048]{2,1,0:T(8,128)(2,1)} %v_far.3, s32[3,8,128]{2,1,0:T(8,128)S(1)} %get-tuple-element.11.rows_ref), custom_call_target="tpu_custom_call" | custom-call | tf_op jit(solution)/shard_map/pallas_call | solution.py:186
  22.9 11.8 %all_to_all.20.blocks_ref = bf16[32,8,128]{2,1,0:T(8,128)(2,1)S(1)} all-to-all(bf16[32,8,128]{2,1,0:T(8,128)(2,1)S(1)} %shard_map.92), channel_id=1, replica_groups=mesh['seq_0'=4,'seq_1'=8,'batch'=16] {'seq_0','seq_1'}, dimensions={0} | all-to-all | bytes 131072 | tf_op jit(solution)/shard_map/all_to_all | solution.py:199
  34.7 0.2 shard_map.93
  34.9 20.7 %all_to_all.21 = bf16[16,4,128]{2,1,0:T(4,128)(2,1)S(1)} all-to-all(bf16[16,4,128]{2,1,0:T(4,128)(2,1)S(1)} %shard_map.93), channel_id=1, replica_groups=mesh['seq_0'=4,'seq_1'=8,'batch'=16] {'batch'}, dimensions={0} | all-to-all | bytes 32768 | tf_op jit(solution)/shard_map/all_to_all | solution.py:219
  55.6 0.0 copy-done
  55.6 0.2 fusion
  55.8 0.1 copy.12
  55.9 12.0 %all_to_all.22 = f32[32,2,288]{2,1,0:T(2,128)S(1)} all-to-all(f32[32,2,288]{2,1,0:T(2,128)S(1)} %copy.12), channel_id=1, replica_groups=mesh['seq_0'=4,'seq_1'=8,'batch'=16] {'seq_0','seq_1'}, dimensions={0} | all-to-all | bytes 147456 | tf_op jit(solution)/shard_map/all_to_all | solution.py:224
  67.9 0.6 reduce_sum.9
Async XLA Ops:
  0.0 55.6 %copy-start = (bf16[128,288]{0,1:T(8,128)(2,1)S(1)}, bf16[128,288]{0,1:T(8,128)(2,1)}, u32[]{:S(2)}) copy-start(bf16[128,288]{0,1:T(8,128)(2,1)} %param.17) | copy-start | bytes 221188
  1.3 19.3 %all-to-all-start = ((bf16[32,4,128]{2,1,0:T(4,128)(2,1)}), bf16[32,4,128]{2,1,0:T(4,128)(2,1)S(1)}, u32[]{:S(2)}, u32[]{:S(2)}) async-start(bf16[32,4,128]{2,1,0:T(4,128)(2,1)} %broadcast_in_dim.2), calls=%async_computation | async-start | bytes 65536 | tf_op jit(solution)/shard_map/all_to_all | solution.py:165

commit v4 on v3

--- a/solution.py
+++ b/solution.py
@@ -3,7 +3,6 @@
 from jax import lax
 from jax.experimental import pallas as pl
 from jax.experimental.pallas import tpu as pltpu
-from jax.sharding import Mesh
 from jax.sharding import PartitionSpec as P
 
 HEADS = 32
@@ -11,7 +10,9 @@
 HD = 128
 QSCALAR = 144
 SCALE = QSCALAR ** (-0.5)
-SEQ = ("seq_0", "seq_1")
+SEQ = "seq"
+BATCH = "batch"
+FIRST = 20
 FLOOR = -1e30
 UNROLL = 4
 
@@ -20,6 +21,12 @@
     request = row & 3
     picked = jnp.where(request == 0, values[0], values[1])
     return jnp.where(request >= 2, jnp.where(request == 2, values[2], values[3]), picked)
+
+
+def exchange(x, axis, first):
+    size = lax.axis_size(axis)
+    order = [(first + i) % size for i in range(size)]
+    return lax.all_to_all(x, axis, 0, 0, axis_index_groups=[order], tiled=True)
 
 
 def fetch_pages(
@@ -81,8 +88,9 @@
 
     def score(i, carry):
         for j in range(UNROLL):
-            k = i * UNROLL + j
-            rows = pl.ds(pl.multiple_of(k * 8, 8), 8)
+            turn = i * UNROLL + j
+            k = (turn + FIRST // 2) % KVH
+            rows = pl.ds(pl.multiple_of(turn * 8, 8), 8)
             cols = pl.ds(pl.multiple_of(k * HD, HD), HD)
             keys = jnp.concatenate([k_ref[i, :, cols] for i in range(4)], axis=1)
             scores_ref[rows] = lax.dot_general(
@@ -110,7 +118,8 @@
         def step(i, carry):
             for j in range(UNROLL):
                 k = i * UNROLL + j
-                rows = pl.ds(pl.multiple_of((base + k) * 8, 8), 8)
+                turn = (base + k + KVH - FIRST // 2) % KVH
+                rows = pl.ds(pl.multiple_of(turn * 8, 8), 8)
                 cols = pl.ds(pl.multiple_of(k * HD, HD), HD)
                 values = jnp.concatenate([held[i, :, cols] for i in range(4)], axis=0)
                 sums = jnp.dot(
@@ -120,8 +129,8 @@
                 sums = sums * stats[:, 3:4]
                 even = jnp.where(row < 4, sums, pltpu.roll(stats, 4, 0))
                 odd = jnp.where(row < 4, pltpu.roll(sums, 4, 0), stats)
-                out_ref[2 * (base + k)] = even.astype(jnp.bfloat16)
-                out_ref[2 * (base + k) + 1] = odd.astype(jnp.bfloat16)
+                out_ref[2 * turn] = even.astype(jnp.bfloat16)
+                out_ref[2 * turn + 1] = odd.astype(jnp.bfloat16)
             return carry
 
         return step
@@ -162,9 +171,7 @@
     def far(x):
         return pltpu.with_memory_space_constraint(x, pltpu.HBM)
 
-    all_queries = lax.all_to_all(
-        jnp.broadcast_to(queries[None], (peers, *queries.shape)), SEQ, 0, 0, tiled=True
-    )
+    all_queries = exchange(jnp.broadcast_to(queries[None], (peers, *queries.shape)), SEQ, FIRST)
     keys, values, rows, own = pl.pallas_call(
         fetch_pages,
         out_shape=(
@@ -196,7 +203,7 @@
         near(all_queries.reshape(HEADS * requests, HD)),
         near(keys), near(values), far(value_cache), near(rows),
     )
-    blocks = lax.all_to_all(blocks, SEQ, 0, 0, tiled=True)
+    blocks = exchange(blocks, SEQ, FIRST)
     attention = pl.pallas_call(
         merge_blocks,
         out_shape=pltpu.VMEM((groups, requests, HD), jnp.bfloat16),
@@ -212,32 +219,31 @@
 ):
     requests = queries.shape[0]
     peers = lax.axis_size(SEQ)
-    groups = lax.axis_size("batch")
+    groups = lax.axis_size(BATCH)
     attention = merged_attention(
         queries, key_cache, value_cache, new_key, new_value, page_table, counts, offsets, groups
     )
-    attention = lax.all_to_all(attention, "batch", 0, 0, tiled=True)
+    attention = exchange(attention, BATCH, FIRST // 2)
     partial = jnp.dot(
         attention.reshape(groups * requests, HD), w_out, preferred_element_type=jnp.float32
     )
     partial = partial.reshape(peers, -1, partial.shape[1])
-    partial = lax.all_to_all(partial, SEQ, 0, 0, tiled=True)
+    partial = exchange(partial, SEQ, FIRST)
     return jnp.sum(partial, axis=0).astype(jnp.bfloat16)
 
 
 def solution(mesh):
-    torus = Mesh(mesh.devices.reshape(4, 8, mesh.shape["batch"]), ("seq_0", "seq_1", "batch"))
     in_specs = (
-        P("batch", SEQ),
-        P("batch", SEQ, None),
-        P("batch", SEQ, None),
-        P("batch", None),
-        P("batch", None),
-        P("batch", SEQ),
-        P("batch", SEQ),
-        P("batch"),
-        P(SEQ, "batch"),
+        P(BATCH, SEQ),
+        P(BATCH, SEQ, None),
+        P(BATCH, SEQ, None),
+        P(BATCH, None),
+        P(BATCH, None),
+        P(BATCH, SEQ),
+        P(BATCH, SEQ),
+        P(BATCH),
+        P(SEQ, BATCH),
     )
     return jax.shard_map(
-        on_device, mesh=torus, in_specs=in_specs, out_specs=P(SEQ, "batch"), check_vma=False
-    )
+        on_device, mesh=mesh, in_specs=in_specs, out_specs=P(SEQ, BATCH), check_vma=False
+    )

time: 68.8 us -> 62.6 us (0.910)
  waiting for transfers between devices: 6.78 us -> 0.01 us
  starting transfers between devices: 10.5 us -> 12.4 us
  blocking collectives: 44.5 us -> 43.2 us
    all_to_all x1, waiting for transfers between devices: 6.78 us -> 0.01 us  [exchange(): return lax.all_to_all(x, axis, 0, 0, axis_index_groups=[order], tiled=True)]
    all_to_all x1, starting transfers between devices: 10.5 us -> 12.4 us  [exchange(): return lax.all_to_all(x, axis, 0, 0, axis_index_groups=[order], tiled=True)]
    all_to_all x3, blocking collectives: 44.5 us -> 43.2 us  [exchange(): return lax.all_to_all(x, axis, 0, 0, axis_index_groups=[order], tiled=True)]
  transfers between devices with their start and end apart: 1 -> 1, of which waited for: 1 -> 0; matrix products, arithmetic and copies ran while one was open for 0% -> 0% of each run, Pallas kernels for 3% -> 3%
where the time goes in v4:
time: 62.6 us; the launch traced here: 62.3 us
  blocking collectives  43.2 us (69%)
  starting transfers between devices  12.4 us (20%)
  Pallas kernels  4.5 us (7%)
  local copies, waits for them, and re-layouts  1.4 us (2%)
    all_to_all x3, blocking collectives, exchange(): return lax.all_to_all(x, axis, 0, 0, axis_index_groups=[order], tiled=True)  43.2 us
    all_to_all x1, starting transfers between devices, exchange(): return lax.all_to_all(x, axis, 0, 0, axis_index_groups=[order], tiled=True)  12.4 us
    pallas_call x1, Pallas kernels, merged_attention(): pl.pallas_call(attend_pages, out_shape=pltpu.VMEM((HEADS, 8, HD), jnp.bfl...  2.31 us
    pallas_call x1, Pallas kernels, merged_attention(): pl.pallas_call(fetch_pages, out_shape=(pltpu.VMEM(key_cache.shape, key_ca...  1.99 us
    broadcast_in_dim x1, local copies, waits for them, and re-layouts, merged_attention(): jnp.broadcast_to(queries[None], (peers, *queries.shape))  1.32 us
  transfers between devices with their start and end apart: 1, of which 0 were waited for; matrix products, arithmetic and copies ran while one was open for 0% of the time, Pallas kernels for 3%

profile of v4, /device:TPU:1, one launch (start us, length us, event | category | flops | bytes accessed | tf_op | source)
XLA Modules:
  0.0 62.3 jit_solution(14209943151816958452)
XLA Ops:
  0.0 0.0 copy-start
  0.0 1.3 %broadcast_in_dim.2 = bf16[32,4,128]{2,1,0:T(4,128)(2,1)} broadcast(bf16[4,128]{1,0:T(4,128)(2,1)} %q_far.1), dimensions={1,2} | broadcast | bytes 33792 | tf_op jit(solution)/shard_map/broadcast_in_dim | solution.py:174
  1.3 12.4 %all-to-all-start = ((bf16[32,4,128]{2,1,0:T(4,128)(2,1)}), bf16[32,4,128]{2,1,0:T(4,128)(2,1)S(1)}, u32[]{:S(2)}, u32[]{:S(2)}) async-start(bf16[32,4,128]{2,1,0:T(4,128)(2,1)} %broadcast_in_dim.2), calls=%async_computation | async-start | bytes 65536 | tf_op jit(solution)/shard_map/all_to_all | solution.py:29
  13.7 2.0 %shard_map.91 = (bf16[4,128,2048]{2,1,0:T(8,128)(2,1)S(1)}, bf16[4,128,1024]{2,1,0:T(8,128)(2,1)S(1)}, s32[3,8,128]{2,1,0:T(8,128)S(1)}, f32[8,128]{1,0:T(8,128)S(1)}) custom-call(s32[4]{0:T(128)} %bitcast.9, s32[4]{0:T(128)} %bitcast.10, s32[4]{0:T(128)} %offsets_far.1, bf16[4,128]{1,0:T(4,128)(2,1)} %q_far.1, bf16[4,2048]{1,0:T(4,128)(2,1)} %new_key_far.1, ...), custom_call_target="tpu_custom_call" | custom-call | tf_op jit(solution)/shard_map/pallas_call | solution.py:175
  15.7 0.0 all-to-all-done
  15.7 2.3 %shard_map.92 = bf16[32,8,128]{2,1,0:T(8,128)(2,1)S(1)} custom-call(bf16[128,128]{1,0:T(8,128)(2,1)S(1)} %bitcast.7, bf16[4,128,2048]{2,1,0:T(8,128)(2,1)S(1)} %get-tuple-element.9.k_ref, bf16[4,128,1024]{2,1,0:T(8,128)(2,1)S(1)} %get-tuple-element.10.v_ref, bf16[4,128,2048]{2,1,0:T(8,128)(2,1)} %v_far.3, s32[3,8,128]{2,1,0:T(8,128)S(1)} %get-tuple-element.11.rows_ref), custom_call_target="tpu_custom_call" | custom-call | tf_op jit(solution)/shard_map/pallas_call | solution.py:193
  18.0 11.7 %all_to_all.20.blocks_ref = bf16[32,8,128]{2,1,0:T(8,128)(2,1)S(1)} all-to-all(bf16[32,8,128]{2,1,0:T(8,128)(2,1)S(1)} %shard_map.92), channel_id=1, replica_groups={{320,336,352,368,384,400,416,432,448,464,480,496,0,16,32,48,64,80,96,11..., dimensions={0} | all-to-all | bytes 131072 | tf_op jit(solution)/shard_map/all_to_all | solution.py:29
  29.7 0.2 shard_map.93
  29.9 18.4 %all_to_all.21 = bf16[16,4,128]{2,1,0:T(4,128)(2,1)S(1)} all-to-all(bf16[16,4,128]{2,1,0:T(4,128)(2,1)S(1)} %shard_map.93), channel_id=1, replica_groups={{10,11,12,13,14,15,0,1,2,3,4,5,6,7,8,9},{26,27,28,29,30,31,16,17,18,19,..., dimensions={0} | all-to-all | bytes 32768 | tf_op jit(solution)/shard_map/all_to_all | solution.py:29
  48.3 0.0 copy-done
  48.3 0.2 fusion
  48.4 0.1 copy.12
  48.5 13.2 %all_to_all.22 = f32[32,2,288]{2,1,0:T(2,128)S(1)} all-to-all(f32[32,2,288]{2,1,0:T(2,128)S(1)} %copy.12), channel_id=1, replica_groups={{320,336,352,368,384,400,416,432,448,464,480,496,0,16,32,48,64,80,96,11..., dimensions={0} | all-to-all | bytes 147456 | tf_op jit(solution)/shard_map/all_to_all | solution.py:29
  61.7 0.6 reduce_sum.9
Async XLA Ops:
  0.0 48.3 %copy-start = (bf16[128,288]{0,1:T(8,128)(2,1)S(1)}, bf16[128,288]{0,1:T(8,128)(2,1)}, u32[]{:S(2)}) copy-start(bf16[128,288]{0,1:T(8,128)(2,1)} %param.17) | copy-start | bytes 221188
  1.3 14.4 %all-to-all-start = ((bf16[32,4,128]{2,1,0:T(4,128)(2,1)}), bf16[32,4,128]{2,1,0:T(4,128)(2,1)S(1)}, u32[]{:S(2)}, u32[]{:S(2)}) async-start(bf16[32,4,128]{2,1,0:T(4,128)(2,1)} %broadcast_in_dim.2), calls=%async_computation | async-start | bytes 65536 | tf_op jit(solution)/shard_map/all_to_all | solution.py:29

commit v5 on v4

--- a/solution.py
+++ b/solution.py
@@ -12,9 +12,12 @@
 SCALE = QSCALAR ** (-0.5)
 SEQ = "seq"
 BATCH = "batch"
-FIRST = 20
+PAIRS = (10, 0, 3, 4, 1, 12, 7, 15, 8, 11, 5, 2, 13, 9, 6, 14)
 FLOOR = -1e30
-UNROLL = 4
+TURNS = tuple(PAIRS.index(k) for k in range(KVH))
+ORDER = tuple(2 * k + i for k in PAIRS for i in range(2))
+UNROLL = 8
+STATS = 3
 
 
 def by_request(row, values):
@@ -23,10 +26,13 @@
     return jnp.where(request >= 2, jnp.where(request == 2, values[2], values[3]), picked)
 
 
-def exchange(x, axis, first):
-    size = lax.axis_size(axis)
-    order = [(first + i) % size for i in range(size)]
-    return lax.all_to_all(x, axis, 0, 0, axis_index_groups=[order], tiled=True)
+def exchange(x, axis, order):
+    return lax.all_to_all(x, axis, 0, 0, axis_index_groups=[list(order)], tiled=True)
+
+
+def looked_up(table, i, j):
+    packed = sum(value << (4 * n) for n, value in enumerate(table[j::UNROLL]))
+    return lax.shift_right_logical(jnp.int32(packed), jnp.int32(4) * i) & 15
 
 
 def fetch_pages(
@@ -89,7 +95,7 @@
     def score(i, carry):
         for j in range(UNROLL):
             turn = i * UNROLL + j
-            k = (turn + FIRST // 2) % KVH
+            k = looked_up(PAIRS, i, j)
             rows = pl.ds(pl.multiple_of(turn * 8, 8), 8)
             cols = pl.ds(pl.multiple_of(k * HD, HD), HD)
             keys = jnp.concatenate([k_ref[i, :, cols] for i in range(4)], axis=1)
@@ -118,7 +124,7 @@
         def step(i, carry):
             for j in range(UNROLL):
                 k = i * UNROLL + j
-                turn = (base + k + KVH - FIRST // 2) % KVH
+                turn = looked_up(TURNS[base : base + KVH // 2], i, j)
                 rows = pl.ds(pl.multiple_of(turn * 8, 8), 8)
                 cols = pl.ds(pl.multiple_of(k * HD, HD), HD)
                 values = jnp.concatenate([held[i, :, cols] for i in range(4)], axis=0)
@@ -127,8 +133,10 @@
                 )
                 stats = stats_ref[rows]
                 sums = sums * stats[:, 3:4]
-                even = jnp.where(row < 4, sums, pltpu.roll(stats, 4, 0))
-                odd = jnp.where(row < 4, pltpu.roll(sums, 4, 0), stats)
+                rest = sums - sums.astype(jnp.bfloat16).astype(jnp.float32)
+                rest = jnp.where(lane < STATS, stats, rest)
+                even = jnp.where(row < 4, sums, pltpu.roll(rest, 4, 0))
+                odd = jnp.where(row < 4, pltpu.roll(sums, 4, 0), rest)
                 out_ref[2 * turn] = even.astype(jnp.bfloat16)
                 out_ref[2 * turn + 1] = odd.astype(jnp.bfloat16)
             return carry
@@ -142,7 +150,8 @@
 
 def merge_blocks(blocks_ref, own_ref, out_ref):
     blocks = blocks_ref[...].astype(jnp.float32)
-    sums = blocks[:, 0:4, :]
+    lane = lax.broadcasted_iota(jnp.int32, (4, HD), 1)
+    sums = blocks[:, 0:4, :] + jnp.where(lane < STATS, 0.0, blocks[:, 4:8, :])
     mark = blocks[:, 4:8, 0:1]
     total = blocks[:, 4:8, 1:2] + blocks[:, 4:8, 2:3]
     new_score = own_ref[0:4, 0:1]
@@ -171,7 +180,7 @@
     def far(x):
         return pltpu.with_memory_space_constraint(x, pltpu.HBM)
 
-    all_queries = exchange(jnp.broadcast_to(queries[None], (peers, *queries.shape)), SEQ, FIRST)
+    all_queries = exchange(jnp.broadcast_to(queries[None], (peers, *queries.shape)), SEQ, ORDER)
     keys, values, rows, own = pl.pallas_call(
         fetch_pages,
         out_shape=(
@@ -203,7 +212,7 @@
         near(all_queries.reshape(HEADS * requests, HD)),
         near(keys), near(values), far(value_cache), near(rows),
     )
-    blocks = exchange(blocks, SEQ, FIRST)
+    blocks = exchange(blocks, SEQ, ORDER)
     attention = pl.pallas_call(
         merge_blocks,
         out_shape=pltpu.VMEM((groups, requests, HD), jnp.bfloat16),
@@ -223,13 +232,13 @@
     attention = merged_attention(
         queries, key_cache, value_cache, new_key, new_value, page_table, counts, offsets, groups
     )
-    attention = exchange(attention, BATCH, FIRST // 2)
+    attention = exchange(attention, BATCH, PAIRS)
     partial = jnp.dot(
         attention.reshape(groups * requests, HD), w_out, preferred_element_type=jnp.float32
     )
-    partial = partial.reshape(peers, -1, partial.shape[1])
-    partial = exchange(partial, SEQ, FIRST)
-    return jnp.sum(partial, axis=0).astype(jnp.bfloat16)
+    partial = partial.astype(jnp.bfloat16).reshape(peers, -1, partial.shape[1])
+    partial = exchange(partial, SEQ, ORDER)
+    return jnp.sum(partial.astype(jnp.float32), axis=0).astype(jnp.bfloat16)
 
 
 def solution(mesh):

time: 62.6 us -> 60.2 us (0.962)
  blocking collectives: 43.2 us -> 41.7 us
  Pallas kernels: 4.5 us -> 3.72 us
    all_to_all x3, blocking collectives: 43.2 us -> 41.7 us  [exchange(): lax.all_to_all(x, axis, 0, 0, axis_index_groups=[list(order)], tiled=True)]
    pallas_call x1, Pallas kernels: 2.31 us -> 1.53 us  [merged_attention(): pl.pallas_call(attend_pages, out_shape=pltpu.VMEM((HEADS, 8, HD), jnp.bfl...]
where the time goes in v5:
time: 60.2 us; the launch traced here: 59.9 us
  blocking collectives  41.7 us (69%)
  starting transfers between devices  12.3 us (20%)
  Pallas kernels  3.72 us (6%)
  local copies, waits for them, and re-layouts  1.36 us (2%)
  other arithmetic  0.63 us (1%)
    all_to_all x3, blocking collectives, exchange(): lax.all_to_all(x, axis, 0, 0, axis_index_groups=[list(order)], tiled=True)  41.7 us
    all_to_all x1, starting transfers between devices, exchange(): lax.all_to_all(x, axis, 0, 0, axis_index_groups=[list(order)], tiled=True)  12.3 us
    pallas_call x1, Pallas kernels, merged_attention(): pl.pallas_call(fetch_pages, out_shape=(pltpu.VMEM(key_cache.shape, key_ca...  1.99 us
    pallas_call x1, Pallas kernels, merged_attention(): pl.pallas_call(attend_pages, out_shape=pltpu.VMEM((HEADS, 8, HD), jnp.bfl...  1.53 us
    broadcast_in_dim x1, local copies, waits for them, and re-layouts, merged_attention(): jnp.broadcast_to(queries[None], (peers, *queries.shape))  1.32 us
  transfers between devices with their start and end apart: 1, of which 0 were waited for; matrix products, arithmetic and copies ran while one was open for 0% of the time, Pallas kernels for 3%

profile of v5, /device:TPU:1, one launch (start us, length us, event | category | flops | bytes accessed | tf_op | source)
XLA Modules:
  0.0 59.9 jit_solution(13567992775945435464)
XLA Ops:
  0.0 0.0 copy-start
  0.0 1.3 %broadcast_in_dim.2 = bf16[32,4,128]{2,1,0:T(4,128)(2,1)} broadcast(bf16[4,128]{1,0:T(4,128)(2,1)} %q_far.1), dimensions={1,2} | broadcast | bytes 33792 | tf_op jit(solution)/shard_map/broadcast_in_dim | solution.py:183
  1.3 12.3 %all-to-all-start = ((bf16[32,4,128]{2,1,0:T(4,128)(2,1)}), bf16[32,4,128]{2,1,0:T(4,128)(2,1)S(1)}, u32[]{:S(2)}, u32[]{:S(2)}) async-start(bf16[32,4,128]{2,1,0:T(4,128)(2,1)} %broadcast_in_dim.2), calls=%async_computation | async-start | bytes 65536 | tf_op jit(solution)/shard_map/all_to_all | solution.py:30
  13.6 2.0 %shard_map.91 = (bf16[4,128,2048]{2,1,0:T(8,128)(2,1)S(1)}, bf16[4,128,1024]{2,1,0:T(8,128)(2,1)S(1)}, s32[3,8,128]{2,1,0:T(8,128)S(1)}, f32[8,128]{1,0:T(8,128)S(1)}) custom-call(s32[4]{0:T(128)} %bitcast.8, s32[4]{0:T(128)} %bitcast.9, s32[4]{0:T(128)} %offsets_far.1, bf16[4,128]{1,0:T(4,128)(2,1)} %q_far.1, bf16[4,2048]{1,0:T(4,128)(2,1)} %new_key_far.1, ...), custom_call_target="tpu_custom_call" | custom-call | tf_op jit(solution)/shard_map/pallas_call | solution.py:184
  15.6 0.0 all-to-all-done
  15.6 1.5 %shard_map.92 = bf16[32,8,128]{2,1,0:T(8,128)(2,1)S(1)} custom-call(bf16[128,128]{1,0:T(8,128)(2,1)S(1)} %bitcast.6, bf16[4,128,2048]{2,1,0:T(8,128)(2,1)S(1)} %get-tuple-element.9.k_ref, bf16[4,128,1024]{2,1,0:T(8,128)(2,1)S(1)} %get-tuple-element.10.v_ref, bf16[4,128,2048]{2,1,0:T(8,128)(2,1)} %v_far.3, s32[3,8,128]{2,1,0:T(8,128)S(1)} %get-tuple-element.11.rows_ref), custom_call_target="tpu_custom_call" | custom-call | tf_op jit(solution)/shard_map/pallas_call | solution.py:202
  17.2 11.6 %all_to_all.20.blocks_ref = bf16[32,8,128]{2,1,0:T(8,128)(2,1)S(1)} all-to-all(bf16[32,8,128]{2,1,0:T(8,128)(2,1)S(1)} %shard_map.92), channel_id=1, replica_groups={{320,336,0,16,96,112,128,144,32,48,384,400,224,240,480,496,256,272,352,..., dimensions={0} | all-to-all | bytes 131072 | tf_op jit(solution)/shard_map/all_to_all | solution.py:30
  28.8 0.2 shard_map.93
  29.0 18.3 %all_to_all.21 = bf16[16,4,128]{2,1,0:T(4,128)(2,1)S(1)} all-to-all(bf16[16,4,128]{2,1,0:T(4,128)(2,1)S(1)} %shard_map.93), channel_id=1, replica_groups={{10,0,3,4,1,12,7,15,8,11,5,2,13,9,6,14},{26,16,19,20,17,28,23,31,24,27,..., dimensions={0} | all-to-all | bytes 32768 | tf_op jit(solution)/shard_map/all_to_all | solution.py:30
  47.3 0.0 copy-done
  47.3 0.2 convolution_convert_fusion
  47.5 11.8 %all_to_all.22 = bf16[32,2,288]{2,1,0:T(2,128)(2,1)S(1)} all-to-all(bf16[32,2,288]{2,1,0:T(2,128)(2,1)S(1)} %reshape.12), channel_id=1, replica_groups={{320,336,0,16,96,112,128,144,32,48,384,400,224,240,480,496,256,272,352,..., dimensions={0} | all-to-all | bytes 73728 | tf_op jit(solution)/shard_map/all_to_all | solution.py:30
  59.3 0.6 %reduce_sum.12 = bf16[2,288]{1,0:T(2,128)(2,1)} reduce(bf16[32,2,288]{2,1,0:T(2,128)(2,1)S(1)} %all_to_all.22, bf16[]{:T(256)} %constant.2.clone.1), dimensions={0}, to_apply=%region_0.0 | reduce | flops 17856 | bytes 38018 | tf_op jit(solution)/shard_map/reduce_sum | solution.py:241
  (1 shorter events, 0.0 us)
Async XLA Ops:
  0.0 47.3 %copy-start = (bf16[128,288]{0,1:T(8,128)(2,1)S(1)}, bf16[128,288]{0,1:T(8,128)(2,1)}, u32[]{:S(2)}) copy-start(bf16[128,288]{0,1:T(8,128)(2,1)} %param.17) | copy-start | bytes 221188
  1.3 14.3 %all-to-all-start = ((bf16[32,4,128]{2,1,0:T(4,128)(2,1)}), bf16[32,4,128]{2,1,0:T(4,128)(2,1)S(1)}, u32[]{:S(2)}, u32[]{:S(2)}) async-start(bf16[32,4,128]{2,1,0:T(4,128)(2,1)} %broadcast_in_dim.2), calls=%async_computation | async-start | bytes 65536 | tf_op jit(solution)/shard_map/all_to_all | solution.py:30

commit v6 on v5

--- a/solution.py
+++ b/solution.py
@@ -12,9 +12,11 @@
 SCALE = QSCALAR ** (-0.5)
 SEQ = "seq"
 BATCH = "batch"
-PAIRS = (10, 0, 3, 4, 1, 12, 7, 15, 8, 11, 5, 2, 13, 9, 6, 14)
+PAIRS = (10, 6, 7, 8, 9, 4, 5, 15, 11, 2, 3, 12, 13, 0, 1, 14)
+SWAP = 7
 FLOOR = -1e30
 TURNS = tuple(PAIRS.index(k) for k in range(KVH))
+GROUPS = (PAIRS[SWAP], *PAIRS[1:SWAP], PAIRS[0], *PAIRS[SWAP + 1 :])
 ORDER = tuple(2 * k + i for k in PAIRS for i in range(2))
 UNROLL = 8
 STATS = 3
@@ -37,7 +39,7 @@
 
 def fetch_pages(
     table_far, counts_far, offsets_far, q_far, new_key_far, new_value_far, k_far, v_far,
-    k_ref, v_ref, rows_ref, own_ref,
+    spread_ref, k_ref, v_ref, rows_ref, own_ref,
     table_ref, counts_ref, offsets_ref, q_ref, new_key_ref, new_value_ref, arrived,
 ):
     place = lax.axis_index(SEQ)
@@ -47,10 +49,10 @@
         pltpu.make_async_copy(source, target, arrived.at[i])
         for i, (source, target) in enumerate(
             (
+                (q_far, q_ref),
                 (table_far, table_ref),
                 (counts_far, counts_ref),
                 (offsets_far, offsets_ref),
-                (q_far, q_ref),
                 (new_key_far.at[:, pl.ds(column, HD)], new_key_ref),
                 (new_value_far.at[:, pl.ds(column, HD)], new_value_ref),
                 (k_far, k_ref),
@@ -63,6 +65,7 @@
     row = lax.broadcasted_iota(jnp.int32, (8, HD), 0)
     for load in loads[:6]:
         load.wait()
+    spread_ref[...] = jnp.broadcast_to(q_ref[...][None], spread_ref.shape)
     rows_ref[0] = by_request(row, [table_ref[r] for r in range(4)])
     rows_ref[1] = by_request(row, [counts_ref[r] for r in range(4)])
     rows_ref[2] = by_request(row, [offsets_ref[r] - place * HD for r in range(4)])
@@ -164,6 +167,14 @@
     out_ref[...] = jnp.broadcast_to(attention[None], out_ref.shape)
 
 
+def project(attention_ref, w_ref, out_ref):
+    blocks = attention_ref[...].astype(jnp.float32)
+    rows = jnp.concatenate([blocks[GROUPS.index(k)] for k in PAIRS]).astype(jnp.bfloat16)
+    out_ref[...] = lax.dot_general(
+        rows, w_ref[...], (((1,), (1,)), ((), ())), preferred_element_type=jnp.float32
+    ).astype(jnp.bfloat16)
+
+
 def merged_attention(
     queries, key_cache, value_cache, new_key, new_value, page_table, counts, offsets, groups
 ):
@@ -180,17 +191,17 @@
     def far(x):
         return pltpu.with_memory_space_constraint(x, pltpu.HBM)
 
-    all_queries = exchange(jnp.broadcast_to(queries[None], (peers, *queries.shape)), SEQ, ORDER)
-    keys, values, rows, own = pl.pallas_call(
+    spread, keys, values, rows, own = pl.pallas_call(
         fetch_pages,
         out_shape=(
+            pltpu.VMEM((peers, *queries.shape), queries.dtype),
             pltpu.VMEM(key_cache.shape, key_cache.dtype),
             pltpu.VMEM(half, value_cache.dtype),
             pltpu.VMEM((3, 8, HD), jnp.int32),
             pltpu.VMEM((8, HD), jnp.float32),
         ),
         in_specs=[hbm] * 8,
-        out_specs=(vmem,) * 4,
+        out_specs=(vmem,) * 5,
         scratch_shapes=[pltpu.SMEM((requests,), jnp.int32)] * 3
         + [pltpu.VMEM((requests, HD), jnp.bfloat16)] * 3
         + [pltpu.SemaphoreType.DMA((8,))],
@@ -199,6 +210,7 @@
         far(page_table[:, 0]), far(counts[:, 0]), far(offsets),
         far(queries), far(new_key), far(new_value), far(key_cache), far(value_cache),
     )
+    all_queries = exchange(spread, SEQ, ORDER)
     blocks = pl.pallas_call(
         attend_pages,
         out_shape=pltpu.VMEM((HEADS, 8, HD), jnp.bfloat16),
@@ -232,11 +244,19 @@
     attention = merged_attention(
         queries, key_cache, value_cache, new_key, new_value, page_table, counts, offsets, groups
     )
-    attention = exchange(attention, BATCH, PAIRS)
-    partial = jnp.dot(
-        attention.reshape(groups * requests, HD), w_out, preferred_element_type=jnp.float32
-    )
-    partial = partial.astype(jnp.bfloat16).reshape(peers, -1, partial.shape[1])
+    attention = exchange(attention, BATCH, GROUPS)
+    vmem = pl.BlockSpec(memory_space=pltpu.VMEM)
+    partial = pl.pallas_call(
+        project,
+        out_shape=pltpu.VMEM((groups * requests, w_out.shape[1]), jnp.bfloat16),
+        in_specs=[vmem] * 2,
+        out_specs=vmem,
+        compiler_params=pltpu.CompilerParams(vmem_limit_bytes=8 << 20),
+    )(
+        pltpu.with_memory_space_constraint(attention, pltpu.VMEM),
+        pltpu.with_memory_space_constraint(w_out.T, pltpu.VMEM),
+    )
+    partial = partial.reshape(peers, -1, partial.shape[1])
     partial = exchange(partial, SEQ, ORDER)
     return jnp.sum(partial.astype(jnp.float32), axis=0).astype(jnp.bfloat16)
 

time: 60.2 us -> 60 us (level)
  blocking collectives: 41.7 us -> 55.2 us
  starting transfers between devices: 12.3 us -> 0 us
  local copies, waits for them, and re-layouts: 1.36 us -> 0.04 us
    all_to_all x3 -> x4, blocking collectives: 41.7 us -> 55.2 us  [exchange(): lax.all_to_all(x, axis, 0, 0, axis_index_groups=[list(order)], tiled=True)]
    all_to_all x1 -> x0, starting transfers between devices: 12.3 us -> none  [exchange(): lax.all_to_all(x, axis, 0, 0, axis_index_groups=[list(order)], tiled=True)]
    broadcast_in_dim x1 -> x0, local copies, waits for them, and re-layouts: 1.32 us -> none  [merged_attention(): jnp.broadcast_to(queries[None], (peers, *queries.shape))]
    pallas_call x1 -> x2, Pallas kernels: 1.99 us -> 2.13 us  [the longest x1 1.97 us: merged_attention(): pl.pallas_call(fetch_pages, out_shape=(pltpu.VMEM((peers, *queries.shape)...]
  transfers between devices with their start and end apart: 1 -> 0, of which waited for: 0 -> 0; matrix products, arithmetic and copies ran while one was open for 0% -> 0% of each run, Pallas kernels for 3% -> 0%
where the time goes in v6:
time: 60 us; the launch traced here: 59.8 us
  blocking collectives  55.2 us (92%)
  Pallas kernels  3.9 us (6%)
  other arithmetic  0.63 us (1%)
    all_to_all x4, blocking collectives, exchange(): lax.all_to_all(x, axis, 0, 0, axis_index_groups=[list(order)], tiled=True)  55.2 us
    pallas_call x1, Pallas kernels, merged_attention(): pl.pallas_call(fetch_pages, out_shape=(pltpu.VMEM((peers, *queries.shape)...  1.97 us
    pallas_call x1, Pallas kernels, merged_attention(): pl.pallas_call(attend_pages, out_shape=pltpu.VMEM((HEADS, 8, HD), jnp.bfl...  1.55 us

profile of v6, /device:TPU:1, one launch (start us, length us, event | category | flops | bytes accessed | tf_op | source)
XLA Modules:
  0.0 59.8 jit_solution(2670369900418662533)
XLA Ops:
  0.0 2.0 %shard_map.91 = (bf16[32,4,128]{2,1,0:T(4,128)(2,1)S(1)}, bf16[4,128,2048]{2,1,0:T(8,128)(2,1)S(1)}, bf16[4,128,1024]{2,1,0:T(8,128)(2,1)S(1)}, s32[3,8,128]{2,1,0:T(8,128)S(1)}, f32[8,128]{1,0:T(8,128)S(1)}) custom-call(s32[4]{0:T(128)} %bitcast.6, s32[4]{0:T(128)} %bitcast.7, s32[4]{0:T(128)} %offsets_far.1, bf16[4,128]{1,0:T(4,128)(2,1)} %q_far.1, ...), custom_call_target="tpu_custom_call" | custom-call | tf_op jit(solution)/shard_map/pallas_call | solution.py:194
  2.0 13.3 %all_to_all.20 = bf16[32,4,128]{2,1,0:T(4,128)(2,1)S(1)} all-to-all(bf16[32,4,128]{2,1,0:T(4,128)(2,1)S(1)} %get-tuple-element.10), channel_id=1, replica_groups={{320,336,192,208,224,240,256,272,288,304,128,144,160,176,480,496,352,36..., dimensions={0} | all-to-all | bytes 65536 | tf_op jit(solution)/shard_map/all_to_all | solution.py:32
  15.3 0.0 copy-start
  15.3 1.6 %shard_map.92 = bf16[32,8,128]{2,1,0:T(8,128)(2,1)S(1)} custom-call(bf16[128,128]{1,0:T(8,128)(2,1)S(1)} %bitcast.4, bf16[4,128,2048]{2,1,0:T(8,128)(2,1)S(1)} %get-tuple-element.11.k_ref, bf16[4,128,1024]{2,1,0:T(8,128)(2,1)S(1)} %get-tuple-element.12.v_ref, bf16[4,128,2048]{2,1,0:T(8,128)(2,1)} %v_far.3, s32[3,8,128]{2,1,0:T(8,128)S(1)} %get-tuple-element.13.rows_ref), custom_call_target="tpu_custom_call" | custom-call | tf_op jit(solution)/shard_map/pallas_call | solution.py:214
  16.8 12.0 %all_to_all.21.blocks_ref = bf16[32,8,128]{2,1,0:T(8,128)(2,1)S(1)} all-to-all(bf16[32,8,128]{2,1,0:T(8,128)(2,1)S(1)} %shard_map.92), channel_id=1, replica_groups={{320,336,192,208,224,240,256,272,288,304,128,144,160,176,480,496,352,36..., dimensions={0} | all-to-all | bytes 131072 | tf_op jit(solution)/shard_map/all_to_all | solution.py:32
  28.8 0.2 shard_map.93
  29.0 18.1 %all_to_all.22.attention_ref = bf16[16,4,128]{2,1,0:T(4,128)(2,1)S(1)} all-to-all(bf16[16,4,128]{2,1,0:T(4,128)(2,1)S(1)} %shard_map.93), channel_id=1, replica_groups={{15,6,7,8,9,4,5,10,11,2,3,12,13,0,1,14},{31,22,23,24,25,20,21,26,27,18,..., dimensions={0} | all-to-all | bytes 32768 | tf_op jit(solution)/shard_map/all_to_all | solution.py:32
  47.1 0.0 copy-done
  47.1 0.2 shard_map.94
  47.3 11.9 %all_to_all.23 = bf16[32,2,288]{2,1,0:T(2,128)(2,1)S(1)} all-to-all(bf16[32,2,288]{2,1,0:T(2,128)(2,1)S(1)} %reshape.7), channel_id=1, replica_groups={{320,336,192,208,224,240,256,272,288,304,128,144,160,176,480,496,352,36..., dimensions={0} | all-to-all | bytes 73728 | tf_op jit(solution)/shard_map/all_to_all | solution.py:32
  59.1 0.6 %reduce_sum.12 = bf16[2,288]{1,0:T(2,128)(2,1)} reduce(bf16[32,2,288]{2,1,0:T(2,128)(2,1)S(1)} %all_to_all.23, bf16[]{:T(256)} %constant.2.clone.1), dimensions={0}, to_apply=%region_0.0 | reduce | flops 17856 | bytes 38018 | tf_op jit(solution)/shard_map/reduce_sum | solution.py:261
  (1 shorter events, 0.0 us)
Async XLA Ops:
  15.3 31.8 %copy-start = (bf16[128,288]{0,1:T(8,128)(2,1)S(1)}, bf16[128,288]{0,1:T(8,128)(2,1)}, u32[]{:S(2)}) copy-start(bf16[128,288]{0,1:T(8,128)(2,1)} %param.17) | copy-start | bytes 221188

commit v7 on v6

--- a/solution.py
+++ b/solution.py
@@ -12,7 +12,7 @@
 SCALE = QSCALAR ** (-0.5)
 SEQ = "seq"
 BATCH = "batch"
-PAIRS = (10, 6, 7, 8, 9, 4, 5, 15, 11, 2, 3, 12, 13, 0, 1, 14)
+PAIRS = (10, 0, 3, 4, 1, 12, 7, 15, 8, 11, 5, 2, 13, 9, 6, 14)
 SWAP = 7
 FLOOR = -1e30
 TURNS = tuple(PAIRS.index(k) for k in range(KVH))

time: 60 us -> 59.8 us (level)
  no operation moved by 1% of the time
where the time goes in v7:
time: 59.8 us; the launch traced here: 59.5 us
  blocking collectives  55 us (92%)
  Pallas kernels  3.9 us (7%)
  other arithmetic  0.63 us (1%)
    all_to_all x4, blocking collectives, exchange(): lax.all_to_all(x, axis, 0, 0, axis_index_groups=[list(order)], tiled=True)  55 us
    pallas_call x1, Pallas kernels, merged_attention(): pl.pallas_call(fetch_pages, out_shape=(pltpu.VMEM((peers, *queries.shape)...  1.97 us
    pallas_call x1, Pallas kernels, merged_attention(): pl.pallas_call(attend_pages, out_shape=pltpu.VMEM((HEADS, 8, HD), jnp.bfl...  1.56 us

profile of v7, /device:TPU:1, one launch (start us, length us, event | category | flops | bytes accessed | tf_op | source)
XLA Modules:
  0.0 59.5 jit_solution(9197706987238408717)
XLA Ops:
  0.0 2.0 %shard_map.91 = (bf16[32,4,128]{2,1,0:T(4,128)(2,1)S(1)}, bf16[4,128,2048]{2,1,0:T(8,128)(2,1)S(1)}, bf16[4,128,1024]{2,1,0:T(8,128)(2,1)S(1)}, s32[3,8,128]{2,1,0:T(8,128)S(1)}, f32[8,128]{1,0:T(8,128)S(1)}) custom-call(s32[4]{0:T(128)} %bitcast.6, s32[4]{0:T(128)} %bitcast.7, s32[4]{0:T(128)} %offsets_far.1, bf16[4,128]{1,0:T(4,128)(2,1)} %q_far.1, ...), custom_call_target="tpu_custom_call" | custom-call | tf_op jit(solution)/shard_map/pallas_call | solution.py:194
  2.0 13.2 %all_to_all.20 = bf16[32,4,128]{2,1,0:T(4,128)(2,1)S(1)} all-to-all(bf16[32,4,128]{2,1,0:T(4,128)(2,1)S(1)} %get-tuple-element.10), channel_id=1, replica_groups={{320,336,0,16,96,112,128,144,32,48,384,400,224,240,480,496,256,272,352,..., dimensions={0} | all-to-all | bytes 65536 | tf_op jit(solution)/shard_map/all_to_all | solution.py:32
  15.2 0.0 copy-start
  15.2 1.6 %shard_map.92 = bf16[32,8,128]{2,1,0:T(8,128)(2,1)S(1)} custom-call(bf16[128,128]{1,0:T(8,128)(2,1)S(1)} %bitcast.4, bf16[4,128,2048]{2,1,0:T(8,128)(2,1)S(1)} %get-tuple-element.11.k_ref, bf16[4,128,1024]{2,1,0:T(8,128)(2,1)S(1)} %get-tuple-element.12.v_ref, bf16[4,128,2048]{2,1,0:T(8,128)(2,1)} %v_far.3, s32[3,8,128]{2,1,0:T(8,128)S(1)} %get-tuple-element.13.rows_ref), custom_call_target="tpu_custom_call" | custom-call | tf_op jit(solution)/shard_map/pallas_call | solution.py:214
  16.8 11.8 %all_to_all.21.blocks_ref = bf16[32,8,128]{2,1,0:T(8,128)(2,1)S(1)} all-to-all(bf16[32,8,128]{2,1,0:T(8,128)(2,1)S(1)} %shard_map.92), channel_id=1, replica_groups={{320,336,0,16,96,112,128,144,32,48,384,400,224,240,480,496,256,272,352,..., dimensions={0} | all-to-all | bytes 131072 | tf_op jit(solution)/shard_map/all_to_all | solution.py:32
  28.6 0.2 shard_map.93
  28.8 18.1 %all_to_all.22.attention_ref = bf16[16,4,128]{2,1,0:T(4,128)(2,1)S(1)} all-to-all(bf16[16,4,128]{2,1,0:T(4,128)(2,1)S(1)} %shard_map.93), channel_id=1, replica_groups={{15,0,3,4,1,12,7,10,8,11,5,2,13,9,6,14},{31,16,19,20,17,28,23,26,24,27,..., dimensions={0} | all-to-all | bytes 32768 | tf_op jit(solution)/shard_map/all_to_all | solution.py:32
  46.9 0.0 copy-done
  46.9 0.2 shard_map.94
  47.1 11.8 %all_to_all.23 = bf16[32,2,288]{2,1,0:T(2,128)(2,1)S(1)} all-to-all(bf16[32,2,288]{2,1,0:T(2,128)(2,1)S(1)} %reshape.7), channel_id=1, replica_groups={{320,336,0,16,96,112,128,144,32,48,384,400,224,240,480,496,256,272,352,..., dimensions={0} | all-to-all | bytes 73728 | tf_op jit(solution)/shard_map/all_to_all | solution.py:32
  58.9 0.6 %reduce_sum.12 = bf16[2,288]{1,0:T(2,128)(2,1)} reduce(bf16[32,2,288]{2,1,0:T(2,128)(2,1)S(1)} %all_to_all.23, bf16[]{:T(256)} %constant.2.clone.1), dimensions={0}, to_apply=%region_0.0 | reduce | flops 17856 | bytes 38018 | tf_op jit(solution)/shard_map/reduce_sum | solution.py:261
  (1 shorter events, 0.0 us)
Async XLA Ops:
  15.2 31.7 %copy-start = (bf16[128,288]{0,1:T(8,128)(2,1)S(1)}, bf16[128,288]{0,1:T(8,128)(2,1)}, u32[]{:S(2)}) copy-start(bf16[128,288]{0,1:T(8,128)(2,1)} %param.17) | copy-start | bytes 221188
